TPU v7x, 32 devices: a whole 2x2x4 slice. The times are simulated.
32 devices in a mesh: gx: 4 (over z), gy: 4 (over x, core), gz: 2 (over y).
Axes of the slice: x: 2, y: 2, z: 4, core: 2. Of those that a mesh axis runs over, the one named last changes fastest.
Arguments:
- charges: bfloat16 [256, 256, 256], P('gx', 'gy', 'gz'), may hold values from -6 to 6
- taps: float32 [4, 4, 17], replicated, may hold values from 0.05 to 0.3
Outputs:
- potential: bfloat16 [256, 256, 256], P('gx', 'gy', 'gz')
All inputs are finite; a program needn't handle non-finite values.
Results may differ from a plain program's by a relative error of at most 0.012.
The roundings to bfloat16 on the way count: a program that leaves them out, or rounds other values in their place, can miss the bound.
Values may be sent and summed in bfloat16 or wider, within the bound.
No kernel may reach another device: no remote copies, remote signals or barrier semaphores. Data moves between devices by JAX's collectives and lax.ppermute only.
A program may use at most 128 MiB of HBM per device.

v0:
```python
import functools

import jax
import jax.numpy as jnp
import numpy as np
from jax import lax
from jax.experimental import pallas as pl
from jax.experimental.pallas import tpu as pltpu
from jax.sharding import PartitionSpec as P

F32, BF16 = jnp.float32, jnp.bfloat16
REACH = 8
LANES = 128
TILE = 16
SLAB = 16
LOW, HIGH = (0, 1, 2, 2), (0, 2, 3, 3)
STENCIL = ((0, 1.0), (-1, 9 / 16), (1, 9 / 16), (-3, -1 / 16), (3, -1 / 16))


def up_to(value, step):
    return -(-value // step) * step


class Level:
    def __init__(self, index, block):
        self.index = index
        self.n = tuple(size >> index for size in block)
        self.low, self.high = LOW[index], HIGH[index]
        self.win = tuple(size + self.low + self.high for size in self.n)
        self.full = tuple(size + 2 * REACH for size in self.win)
        self.out = tuple(up_to(size, TILE) for size in self.win[:2])
        self.inp = tuple(size + TILE for size in self.out)
        self.rows = up_to(self.win[1], 8)
        self.lane = 0
        self.start = 0
        self.span = up_to(self.full[0] * self.inp[1], LANES)


def levels_of(block):
    levels = [Level(index, block) for index in range(4)]
    lane, start = 0, 0
    for level in levels[1:]:
        level.lane, level.start = lane, start
        lane += level.win[2]
        start += level.span
    assert lane <= LANES and block[2] == LANES
    assert all(level.n[d] % 8 == 0 for level in levels for d in range(3))
    return levels


def own_lane(level, z):
    return (level.lane + z + level.low + REACH) % LANES


def restrict_rows(coarse, fine):
    fine_rows = fine.n[1] if fine.index == 0 else fine.rows
    matrix = np.zeros((coarse.rows, 2, fine_rows))
    for row in range(coarse.win[1]):
        for offset, weight in STENCIL:
            col = 2 * (row - coarse.low) + offset + fine.low
            if 0 <= col < fine.win[1]:
                matrix[row, :, col] = weight
    return matrix.reshape(coarse.rows, 2 * fine_rows)


def restrict_lanes(coarse, fine):
    matrix = np.zeros((2, LANES, LANES))
    for z in range(-coarse.low, coarse.n[2] + coarse.high):
        for offset, weight in STENCIL:
            at = 2 * z + offset
            if -fine.low <= at < fine.n[2] + fine.high:
                lane = at if fine.index == 0 else own_lane(fine, at)
                matrix[:, lane, own_lane(coarse, z)] = weight
    return matrix.reshape(2 * LANES, LANES)


def prolong_weights(fine_at):
    half = fine_at // 2
    if fine_at % 2 == 0:
        return ((half, 1.0),)
    return ((half, 9 / 16), (half + 1, 9 / 16), (half - 1, -1 / 16), (half + 2, -1 / 16))


def prolong_matrix(fine_count, fine_win, fine_low, coarse_count, coarse_low):
    matrix = np.zeros((fine_count, coarse_count))
    for row in range(fine_win):
        for at, weight in prolong_weights(row - fine_low):
            if 0 <= at + coarse_low < coarse_count:
                matrix[row, at + coarse_low] = weight
    return matrix


def prolong_rows(fine, coarse):
    matrix = prolong_matrix(fine.out[1], fine.win[1], fine.low, coarse.out[1], coarse.low)
    return np.concatenate([matrix, matrix], 1)


def prolong_lanes(fine, coarse):
    matrix = prolong_matrix(LANES, fine.win[2], fine.low, LANES, coarse.low).T
    return np.concatenate([matrix, matrix], 0)


def send_lanes(level):
    up, down = np.zeros((SLAB, LANES)), np.zeros((SLAB, LANES))
    for j in range(SLAB):
        s = level.n[2] - REACH + j
        if s < level.win[2]:
            up[j, own_lane(level, s - level.low)] = 1
        if j < level.low + level.high + REACH:
            down[j, own_lane(level, j - level.low)] = 1
    return np.concatenate([up, down], 0)


def place_lanes(level):
    from_prev, from_next = np.zeros((SLAB, LANES)), np.zeros((SLAB, LANES))
    for j in range(SLAB):
        if level.n[2] - REACH + j < level.win[2]:
            from_prev[j, (level.lane + j) % LANES] = 1
        at = j + REACH + level.n[2]
        if at < level.full[2]:
            from_next[j, (level.lane + at) % LANES] = 1
    return np.concatenate([from_prev, from_next] * (1 if level.index == 1 else 2), 0)


def dot(a, b, dims=((1,), (0,))):
    return lax.dot_general(a, b, (dims, ((), ())), preferred_element_type=F32)


def split_rows(x):
    high = x.astype(BF16).astype(F32)
    return jnp.concatenate([high, x - high], 0).astype(BF16)


def split_lanes(x):
    high = x.astype(BF16).astype(F32)
    return jnp.concatenate([high, x - high], 1).astype(BF16)


class Table:
    def __init__(self):
        self.parts, self.places, self.count = [], {}, 0

    def add(self, key, matrix):
        rows, cols = matrix.shape
        padded = np.zeros((up_to(rows, TILE), LANES), np.float32)
        padded[:rows, :cols] = matrix
        self.places[key] = (self.count, rows, cols)
        self.parts.append(padded)
        self.count += padded.shape[0]

    def array(self):
        return jnp.asarray(np.concatenate(self.parts, 0), BF16)

    def get(self, ref, *key):
        start, rows, cols = self.places[key]
        return ref[start : start + rows, :cols]


def pad_rows(x, rows):
    if x.shape[0] == rows:
        return x
    return jnp.concatenate([x, jnp.zeros((rows - x.shape[0], x.shape[1]), x.dtype)], 0)


def total(terms):
    return functools.reduce(lambda a, b: a + b, terms)


def bands_kernel(levels, taps_ref, band_ref, lanes_ref):
    row = lax.broadcasted_iota(jnp.int32, (8 * TILE, 16 * TILE), 0)
    col = lax.broadcasted_iota(jnp.int32, (8 * TILE, 16 * TILE), 1)
    offset = jnp.where(row % 8 == col // 32, col % 32 - row // 8, -1)

    @pl.loop(0, 16)
    def _(which):
        matrix = jnp.zeros(offset.shape, F32)
        for tap in range(17):
            matrix = jnp.where(offset == tap, taps_ref[which, tap], matrix)
        band_ref[which] = matrix.astype(BF16)

    for level in levels:
        first, count = lane_rows(level)
        k = lax.broadcasted_iota(jnp.int32, (count, LANES), 0)
        z_out = lax.broadcasted_iota(jnp.int32, (count, LANES), 1)
        if level.index == 0:
            n = level.n[2]
            z_in = jnp.where(k < n, k + REACH, jnp.where(k < n + REACH, k - n, k))
            valid = k < n + 2 * REACH
        else:
            z_in = (k + (LANES - level.lane)) % LANES
            valid = (z_in < level.full[2]) & (z_out < level.win[2])
        offset_z = jnp.where(valid, z_in - z_out, -1)
        for term in range(4):
            matrix = jnp.zeros(offset_z.shape, F32)
            for tap in range(17):
                matrix = jnp.where(offset_z == tap, taps_ref[4 * level.index + term, tap], matrix)
            lanes_ref[first : first + count, term_lanes(term)] = matrix.astype(BF16)


def lane_rows(level):
    return (0, 2 * LANES) if level.index == 0 else ((level.index + 1) * LANES, LANES)


def term_lanes(term):
    return slice(term * LANES, (term + 1) * LANES)


def plane_at(levels, level, which, rows):
    first = 0
    for other in levels[1:]:
        sizes = (other.win[0], other.rows) if rows == "own" else (other.full[0], other.rows)
        if other is level:
            return slice(first + which * sizes[1], first + (which + 1) * sizes[1])
        first += sizes[0] * sizes[1]
    return first


def halves_of(x):
    high = x.astype(BF16).astype(F32)
    return high, x - high


def restrict_kernel(levels, table, charges_ref, table_ref, q_ref, up_ref, down_ref, far_ref):
    for level, fine in zip(levels[1:], levels[:3]):
        for at in range(level.win[0]):
            terms = {}
            for offset, weight in STENCIL:
                plane = 2 * (at - level.low) + offset + fine.low
                if 0 <= plane < fine.win[0]:
                    if fine.index == 0:
                        value = charges_ref[plane].astype(F32)
                    else:
                        value = q_ref[plane_at(levels, fine, plane, "own")]
                    terms.setdefault(weight, []).append(value)
            value = total([total(group) * weight for weight, group in terms.items()])
            value = dot(table.get(table_ref, "rows", level.index), split_rows(value))
            value = dot(split_lanes(value), table.get(table_ref, "lanes", level.index))
            q_ref[plane_at(levels, level, at, "own")] = value
    rows, rest_rows = levels[1].rows, levels[2].rows
    for j in range(up_ref.shape[0]):
        for slab_ref, bases in ((up_ref, [lv.n[0] - REACH for lv in levels[1:]]), (down_ref, [0] * 3)):
            highs, rests = [], [jnp.zeros((rest_rows, LANES), F32)]
            for level, base in zip(levels[1:], bases):
                if base + j < level.win[0]:
                    high, rest = halves_of(q_ref[plane_at(levels, level, base + j, "own")])
                    highs.append(pad_rows(high, rows))
                    if level.index > 1:
                        rests.append(pad_rows(rest, rest_rows))
            slab_ref[j] = jnp.concatenate([total(highs), total(rests)], 0).astype(BF16)
    last = levels[3]
    pack_far(
        far_ref,
        [q_ref[plane_at(levels, last, at, "own")] for at in range(last.win[0])],
    )


def pack_far(far_ref, planes):
    for group in range(far_ref.shape[0]):
        members = planes[4 * group : 4 * group + 4]
        far_ref[group] = total(
            [pltpu.roll(x, 32 * k, 1) if k else x for k, x in enumerate(members)]
        )


def unpack_far(far_ref, at):
    x = far_ref[at // 4]
    return pltpu.roll(x, LANES - 32 * (at % 4), 1) if at % 4 else x


def lane_masks(levels):
    lane = lax.broadcasted_iota(jnp.int32, (8, LANES), 1)
    masks = []
    for level in levels[1:]:
        at = (lane + (2 * LANES - level.lane - REACH)) % LANES
        masks.append((at < level.win[2])[:1])
    return masks


def rows_kernel(levels, q_ref, prev_ref, next_ref, far_prev_ref, *refs):
    far_next_ref = far_prev_ref if len(refs) == 4 else refs[0]
    x_ref, up_ref, down_ref, far_ref = refs[-4:]
    count, high_rows = prev_ref.shape[0], levels[1].rows
    masks = lane_masks(levels)
    coarsest = []

    def received(ref, at, level):
        slab = ref[at].astype(F32)
        high = slab[: level.rows]
        return high if level.index == 1 else high + slab[high_rows : high_rows + level.rows]

    rest_count = levels[2].full[0]
    for at in range(levels[1].full[0]):
        ups, downs = [], []
        for level, mask in zip(levels[1:], masks):
            if at >= level.full[0]:
                continue
            n = level.n[0]
            terms = []
            if 0 <= at - REACH < level.win[0]:
                terms.append(q_ref[plane_at(levels, level, at - REACH, "own")])
            if at < count and at - REACH + n < level.win[0]:
                terms.append(received(prev_ref, at, level))
            if 0 <= at - REACH - n < count:
                terms.append(received(next_ref, at - REACH - n, level))
            if level.index == 3:
                if at - REACH + 2 * n < level.win[0]:
                    terms.append(unpack_far(far_prev_ref, at - REACH + 2 * n))
                if at - REACH - 2 * n >= 0:
                    terms.append(unpack_far(far_next_ref, at - REACH - 2 * n))
            value = jnp.where(mask, total(terms), 0.0)
            x_ref[plane_at(levels, level, at, "full")] = value
            first = level.n[1] - REACH
            ups.append((level.index, halves_of(value[first : first + SLAB])))
            downs.append((level.index, halves_of(value[:SLAB])))
            if level.index == 3:
                coarsest.append(value)
        for slab_ref, parts in ((up_ref, ups), (down_ref, downs)):
            slab_ref[at] = total([x for _, (x, _) in parts]).astype(BF16)
            rests = [x for index, (_, x) in parts if index > 1]
            if rests:
                slab_ref[levels[1].full[0] + at] = total(rests).astype(BF16)
    pack_far(far_ref, coarsest)


def lanes_kernel(levels, table, x_ref, prev_ref, next_ref, far_prev_ref, *refs):
    far_next_ref = far_prev_ref if len(refs) == 3 else refs[0]
    table_ref, flat_ref, slab_ref = refs[-3:]

    def received(ref, at, level):
        high = ref[at].astype(F32)
        return high if level.index == 1 else high + ref[levels[1].full[0] + at].astype(F32)

    for level, mask in zip(levels[1:], lane_masks(levels)):
        blocks, step = level.inp[1] // 8, level.n[1] // 8
        for at in range(level.full[0]):
            own = x_ref[plane_at(levels, level, at, "full")]
            slabs = [received(prev_ref, at, level), received(next_ref, at, level)]
            if level.index == 3:
                slabs += [unpack_far(far_prev_ref, at), unpack_far(far_next_ref, at)]
            parts = []
            for block in range(blocks):
                terms = []
                if 0 <= block - 1 < level.rows // 8:
                    terms.append(own[8 * block - 8 : 8 * block])
                places = [block, block - 1 - step, block - 1 + 2 * step, block - 1 - 2 * step]
                for slab, place in zip(slabs, places):
                    if 0 <= place < SLAB // 8:
                        terms.append(slab[8 * place : 8 * place + 8])
                parts.append(total(terms) if terms else jnp.zeros((8, LANES), F32))
            value = jnp.where(mask, jnp.concatenate(parts, 0), 0.0)
            first = level.start + at * level.inp[1]
            flat_ref[first : first + level.inp[1]] = value
        used = level.start + level.full[0] * level.inp[1]
        last = level.start + level.span
        if used < last:
            flat_ref[used:last] = jnp.zeros((last - used, LANES), F32)
    shift = levels[-1].start + levels[-1].span - levels[2].start
    for level in levels[1:]:
        send = table.get(table_ref, "send", level.index)
        for first in range(level.start, level.start + level.span, 512):
            stop = min(first + 512, level.start + level.span)
            high, rest = halves_of(flat_ref[first:stop])
            slab_ref[:, first:stop] = dot(send, high.astype(BF16), ((1,), (1,))).astype(BF16)
            if level.index > 1:
                slab_ref[:, first + shift : stop + shift] = dot(
                    send, rest.astype(BF16), ((1,), (1,))
                ).astype(BF16)


def halo_kernel(wide_ref, out_ref):
    planes, rows, count = wide_ref.shape
    row = lax.broadcasted_iota(jnp.int32, (2 * REACH, count), 0)
    lane = lax.broadcasted_iota(jnp.int32, (2 * REACH, count), 1)
    send = jnp.where(lane == (row + (count - REACH)) % count, 1.0, 0.0).astype(BF16)
    step = 8
    for first in range(0, planes, step):
        chunk = wide_ref[first : first + step].reshape(step * rows, LANES)
        out_ref[:, first * rows : (first + step) * rows] = dot(send, chunk, ((1,), (1,))).astype(BF16)


def two_passes(level, band, first_ref, second_ref, put):
    def parts_of(result):
        parts = [result[:, :LANES], result[:, LANES:]]
        return jnp.concatenate([x.reshape(TILE, 8, LANES) for x in parts], 1)

    def along_y(pair):
        for block in range(level.out[1] // TILE):
            for term in range(4):
                halves = [
                    first_ref[
                        pl.ds(pair * 16 + 8 * half, 8),
                        TILE * block : TILE * block + 32,
                        term_lanes(term),
                    ].reshape(256, LANES)
                    for half in range(2)
                ]
                result = dot(band(term), jnp.concatenate(halves, 1))
                second_ref[
                    term, TILE * block : TILE * (block + 1), pl.ds(pl.multiple_of(pair * 16, 16), 16)
                ] = parts_of(result).astype(BF16)

    def along_x(pair):
        for block in range(level.out[0] // TILE):
            result = None
            for term in range(4):
                halves = [
                    second_ref[
                        term, pl.ds(pair * 16 + 8 * half, 8), TILE * block : TILE * block + 32
                    ].reshape(256, LANES)
                    for half in range(2)
                ]
                part = dot(band(term), jnp.concatenate(halves, 1))
                result = part if result is None else result + part
            put(block, pair, parts_of(result))

    pl.loop(0, level.inp[0] // 16)(along_y)
    pl.loop(0, level.out[1] // 16)(along_x)


def fine_kernel(level, wide_ref, halo_ref, lanes_ref, band_ref, out_ref, first_ref, second_ref):
    rows, step = level.inp[1], 8
    row = lax.broadcasted_iota(jnp.int32, (2 * REACH, LANES), 0)
    lane = lax.broadcasted_iota(jnp.int32, (2 * REACH, LANES), 1)
    place = jnp.where(lane == row, 1.0, 0.0).astype(BF16)

    @pl.loop(0, level.inp[0] // step)
    def _(chunk):
        where = pl.ds(pl.multiple_of(chunk * step * rows, LANES), step * rows)
        sides = dot(halo_ref[:, where], place, ((0,), (0,))).astype(BF16)
        here = wide_ref[pl.ds(chunk * step, step)].reshape(step * rows, LANES)
        result = dot(jnp.concatenate([here, sides], 1), lanes_ref[: 2 * LANES])
        first_ref[pl.ds(chunk * step, step)] = result.astype(BF16).reshape(step, rows, 4 * LANES)

    def put(block, pair, value):
        out_ref[TILE * block : TILE * (block + 1), pl.ds(pl.multiple_of(pair * 16, 16), 16)] = value

    two_passes(level, lambda term: band_ref[term], first_ref, second_ref, put)


def coarse_kernel(levels, table, flat_ref, slab_ref, lanes_ref, band_ref, table_ref, fine_ref, *refs):
    out_ref, first_refs, second_refs, sum_refs = refs[0], refs[1:4], refs[4:7], refs[7:10]
    shift = levels[-1].start + levels[-1].span - levels[2].start
    for level in reversed(levels[1:]):
        which = level.index - 1
        first_ref, sum_ref = first_refs[which], sum_refs[which]
        rows, step = level.inp[1], 4
        first_lane, _ = lane_rows(level)
        place = table.get(table_ref, "place", level.index)
        for plane in range(0, level.full[0], step):
            count = min(step, level.full[0] - plane)
            if (count * rows) % LANES:
                count += 1
            start, stop = level.start + plane * rows, level.start + (plane + count) * rows
            slab = slab_ref[:, start:stop]
            if level.index > 1:
                slab = jnp.concatenate([slab, slab_ref[:, start + shift : stop + shift]], 0)
            value = flat_ref[start:stop] + dot(slab, place, ((0,), (0,)))
            result = dot(value.astype(BF16), lanes_ref[first_lane : first_lane + LANES])
            first_ref[plane : plane + count] = result.astype(BF16).reshape(count, rows, 4 * LANES)
        rest = level.inp[0] - plane - count
        if rest > 0:
            first_ref[plane + count :] = jnp.zeros((rest, rows, 4 * LANES), BF16)

        def put(block, pair, value, sum_ref=sum_ref):
            sum_ref[TILE * block : TILE * (block + 1), pl.ds(pl.multiple_of(pair * 16, 16), 16)] = value

        base = 4 * level.index
        two_passes(level, lambda term, base=base: band_ref[base + term], first_ref, second_refs[which], put)

    def stretch(fine, coarse, source):
        planes, rows, _ = source.shape
        for first in range(0, coarse.win[0], 4):
            count = min(4, planes - first)
            value = split_lanes(source[first : first + count].reshape(count * rows, LANES))
            value = dot(value, table.get(table_ref, "zed", fine.index))
            source[first : first + count] = value.reshape(count, rows, LANES)

    def prolong(fine, coarse, halves, source, emit):
        planes = []
        for half in halves:
            at = half + coarse.low
            between = (9.0 * (source[at] + source[at + 1]) - (source[at - 1] + source[at + 2])) / 16.0
            planes += [split_rows(source[at]), split_rows(between)]
        both = dot(table.get(table_ref, "tall", fine.index), jnp.concatenate(planes, 1))
        for k, half in enumerate(halves):
            emit(2 * half, both[:, 2 * k * LANES : (2 * k + 1) * LANES])
            emit(2 * half + 1, both[:, (2 * k + 1) * LANES : (2 * k + 2) * LANES])

    for fine, coarse in ((levels[2], levels[3]), (levels[1], levels[2])):
        sum_ref = sum_refs[fine.index - 1]
        source = sum_refs[coarse.index - 1]
        stretch(fine, coarse, source)

        def emit(at, value, fine=fine, sum_ref=sum_ref):
            plane = at + fine.low
            if 0 <= plane < fine.win[0]:
                sum_ref[plane] = sum_ref[plane] + value

        for half in range(-1, (fine.n[0] + fine.high + 1) // 2):
            prolong(fine, coarse, [half], source, emit)

    stretch(levels[0], levels[1], sum_refs[0])

    @pl.loop(0, levels[0].n[0] // 8)
    def _(group):
        def emit(at, value):
            out_ref[at] = (fine_ref[at] + value).astype(BF16)

        prolong(levels[0], levels[1], [4 * group + k for k in range(4)], sum_refs[0], emit)


def make_table(levels):
    table = Table()
    for level, fine in zip(levels[1:], levels[:3]):
        table.add(("rows", level.index), restrict_rows(level, fine))
        table.add(("lanes", level.index), restrict_lanes(level, fine))
        table.add(("send", level.index), send_lanes(level))
        table.add(("place", level.index), place_lanes(level))
        table.add(("tall", fine.index), prolong_rows(fine, level))
        table.add(("zed", fine.index), prolong_lanes(fine, level))
    return table


def call(kernel, out_shape, args, scratch=(), smem=(), flops=0, limit=12):
    specs = [
        pl.BlockSpec(memory_space=pltpu.SMEM if i in smem else pltpu.VMEM) for i in range(len(args))
    ]
    single = not isinstance(out_shape, (list, tuple))
    outs = [out_shape] if single else list(out_shape)
    out_specs = [pl.BlockSpec(memory_space=pltpu.VMEM) for _ in outs]
    return pl.pallas_call(
        kernel,
        out_shape=out_shape,
        in_specs=specs,
        out_specs=out_specs[0] if single else out_specs,
        scratch_shapes=list(scratch),
        compiler_params=pltpu.CompilerParams(vmem_limit_bytes=limit << 20),
        cost_estimate=pl.CostEstimate(flops=flops, bytes_accessed=1 << 20, transcendentals=0),
    )(*args)


def shape(sizes, dtype):
    return jax.ShapeDtypeStruct(tuple(sizes), dtype)


def shifted(value, axis, by):
    count = lax.axis_size(axis)
    return lax.ppermute(value, axis, [(i, (i + by) % count) for i in range(count)])


def far_pair(value, axis):
    after = shifted(value, axis, 2)
    return [after] if lax.axis_size(axis) == 4 else [after, shifted(value, axis, -2)]


def z_pair(value, axis):
    half = value.shape[0] // 2
    if lax.axis_size(axis) == 2:
        return shifted(value, axis, 1)
    return jnp.concatenate([shifted(value[:half], axis, 1), shifted(value[half:], axis, -1)], 0)


def per_device(charges, taps):
    levels = levels_of(charges.shape)
    table = make_table(levels)
    table_array = table.array()
    zero, coarse = levels[0], levels[1:]
    reach = REACH

    x_prev = shifted(charges[-reach:], "gx", 1)
    x_next = shifted(charges[:reach], "gx", -1)

    slab_planes = max(level.low + level.high + reach for level in coarse)
    slab_rows = levels[1].rows + levels[2].rows
    q, l_up, l_down, l_far = call(
        functools.partial(restrict_kernel, levels, table),
        [shape((sum(lv.win[0] * lv.rows for lv in coarse), LANES), F32)]
        + [shape((slab_planes, slab_rows, LANES), BF16)] * 2
        + [shape((up_to(levels[3].win[0], 4) // 4, SLAB, LANES), F32)],
        [charges, table_array],
        flops=1 << 27,
    )
    band, lanes = call(
        functools.partial(bands_kernel, levels),
        [shape((16, 8 * TILE, 16 * TILE), BF16), shape((5 * LANES, 4 * LANES), BF16)],
        [taps.reshape(16, 17)],
        smem=(0,),
        flops=1 << 26,
    )

    l_prev = shifted(l_up, "gx", 1)
    l_next = shifted(l_down, "gx", -1)
    far = far_pair(l_far, "gx")

    pieces = (x_prev, charges, x_next)
    y_prev = shifted(jnp.concatenate([x[:, -reach:] for x in pieces], 0), "gy", 1)
    y_next = shifted(jnp.concatenate([x[:, :reach] for x in pieces], 0), "gy", -1)

    r, m_up, m_down, m_far = call(
        functools.partial(rows_kernel, levels),
        [shape((sum(lv.full[0] * lv.rows for lv in coarse), LANES), F32)]
        + [shape((levels[1].full[0] + levels[2].full[0], SLAB, LANES), BF16)] * 2
        + [shape((up_to(levels[3].full[0], 4) // 4, SLAB, LANES), F32)],
        [q, l_prev, l_next, *far],
        flops=1 << 25,
    )
    m_prev = shifted(m_up, "gy", 1)
    m_next = shifted(m_down, "gy", -1)
    far = far_pair(m_far, "gy")

    wide = jnp.concatenate([y_prev, jnp.concatenate(pieces, 0), y_next], 1)
    sides = call(
        halo_kernel,
        shape((2 * reach, wide.shape[0] * wide.shape[1]), BF16),
        [wide],
        flops=1 << 26,
    )
    halo = z_pair(sides, "gz")

    flat_rows = sum(level.span for level in coarse)
    flat, slabs = call(
        functools.partial(lanes_kernel, levels, table),
        [
            shape((flat_rows, LANES), F32),
            shape((2 * SLAB, 2 * flat_rows - levels[1].span), BF16),
        ],
        [r, m_prev, m_next, *far, table_array],
        flops=1 << 26,
    )
    slabs = z_pair(slabs, "gz")

    fine = call(
        functools.partial(fine_kernel, zero),
        shape(charges.shape, F32),
        [wide, halo, lanes, band],
        scratch=[
            pltpu.VMEM((*zero.inp, 4 * LANES), BF16),
            pltpu.VMEM((4, zero.out[1], zero.inp[0], LANES), BF16),
        ],
        flops=1 << 32,
        limit=24,
    )
    return call(
        functools.partial(coarse_kernel, levels, table),
        shape(charges.shape, BF16),
        [flat, slabs, lanes, band, table_array, fine],
        scratch=[pltpu.VMEM((*lv.inp, 4 * LANES), BF16) for lv in coarse]
        + [pltpu.VMEM((4, lv.out[1], lv.inp[0], LANES), BF16) for lv in coarse]
        + [pltpu.VMEM((*lv.out, LANES), F32) for lv in coarse],
        flops=1 << 31,
        limit=30,
    )


def solution(mesh):
    return jax.shard_map(
        per_device,
        mesh=mesh,
        in_specs=(P("gx", "gy", "gz"), P()),
        out_specs=P("gx", "gy", "gz"),
        check_vma=False,
    )
```

profile of v0, /device:TPU:0, one launch (start us, length us, event | category | flops | bytes accessed | tf_op | source)
XLA Modules:
  0.0 67.4 jit_solution(7214927565824993072)
XLA Ops:
  0.0 1.0 %fusion.1 = (bf16[8,64,128]{2,1,0:T(8,128)(2,1)S(1)}, bf16[8,64,128]{2,1,0:T(8,128)(2,1)S(1)}) fusion(bf16[64,64,128]{2,1,0:T(8,128)(2,1)} %charges_ref.1), kind=kLoop, calls=%fused_computation.4 | loop fusion | bytes 524288 | tf_op jit(solution)/shard_map/slice | solution.py:570
  1.0 3.1 %collective-permute-start.7 = (bf16[8,64,128]{2,1,0:T(8,128)(2,1)S(1)}, bf16[8,64,128]{2,1,0:T(8,128)(2,1)S(1)}, u32[]{:S(2)}, u32[]{:S(2)}) collective-permute-start(bf16[8,64,128]{2,1,0:T(8,128)(2,1)S(1)} %get-tuple-element.31), channel_id=1, source_target_pairs={{0,8},{8,16},{16,24},{24,0},{1,9},{9,17},{17,25},{25,1},{2,10},{10... | collective-permute-start | bytes 393224 | tf_op jit(solution)/shard_map/ppermute | solution.py:548
  4.1 2.1 %collective-permute-start.8 = (bf16[8,64,128]{2,1,0:T(8,128)(2,1)S(1)}, bf16[8,64,128]{2,1,0:T(8,128)(2,1)S(1)}, u32[]{:S(2)}, u32[]{:S(2)}) collective-permute-start(bf16[8,64,128]{2,1,0:T(8,128)(2,1)S(1)} %get-tuple-element.32), channel_id=1, source_target_pairs={{0,24},{8,0},{16,8},{24,16},{1,25},{9,1},{17,9},{25,17},{2,26},{10... | collective-permute-start | bytes 393224 | tf_op jit(solution)/shard_map/ppermute | solution.py:548
  6.2 0.0 copy-start
  6.2 1.2 %copy-done = bf16[64,64,128]{2,1,0:T(8,128)(2,1)S(1)} copy-done((bf16[64,64,128]{2,1,0:T(8,128)(2,1)S(1)}, bf16[64,64,128]{2,1,0:T(8,128)(2,1)}, u32[]{:S(2)}) %copy-start) | copy-done | bytes 1048600
  7.4 0.0 copy-start.2
  7.4 1.0 %copy-done.2 = bf16[2032,128]{1,0:T(8,128)(2,1)S(1)} copy-done((bf16[2032,128]{1,0:T(8,128)(2,1)S(1)}, bf16[2032,128]{1,0:T(8,128)(2,1)}, u32[]{:S(2)}) %copy-start.2) | copy-done | bytes 520216
  8.5 0.0 copy-start.1
  8.5 2.9 %shard_map.37 = (f32[2112,128]{1,0:T(8,128)S(1)}, bf16[13,64,128]{2,1,0:T(8,128)(2,1)S(1)}, bf16[13,64,128]{2,1,0:T(8,128)(2,1)S(1)}, f32[4,16,128]{2,1,0:T(8,128)S(1)}) custom-call(bf16[64,64,128]{2,1,0:T(8,128)(2,1)S(1)} %copy-done, bf16[2032,128]{1,0:T(8,128)(2,1)S(1)} %copy-done.2), custom_call_target="tpu_custom_call" | custom-call | flops 134217728 | bytes 1048576 | tf_op jit(solution)/shard_map/pallas_call | solution.py:531
  11.4 1.0 %collective-permute-start.2 = (f32[4,16,128]{2,1,0:T(8,128)S(1)}, f32[4,16,128]{2,1,0:T(8,128)S(1)}, u32[]{:S(2)}, u32[]{:S(2)}) collective-permute-start(f32[4,16,128]{2,1,0:T(8,128)S(1)} %get-tuple-element.20), channel_id=1, source_target_pairs={{0,16},{8,24},{16,0},{24,8},{1,17},{9,25},{17,1},{25,9},{2,18},{10... | collective-permute-start | bytes 98312 | tf_op jit(solution)/shard_map/ppermute | solution.py:548
  12.4 1.6 %collective-permute-start = (bf16[13,64,128]{2,1,0:T(8,128)(2,1)S(1)}, bf16[13,64,128]{2,1,0:T(8,128)(2,1)S(1)}, u32[]{:S(2)}, u32[]{:S(2)}) collective-permute-start(bf16[13,64,128]{2,1,0:T(8,128)(2,1)S(1)} %get-tuple-element.18), channel_id=1, source_target_pairs={{0,8},{8,16},{16,24},{24,0},{1,9},{9,17},{17,25},{25,1},{2,10},{10... | collective-permute-start | bytes 638984 | tf_op jit(solution)/shard_map/ppermute | solution.py:548
  14.0 2.2 %collective-permute-start.1 = (bf16[13,64,128]{2,1,0:T(8,128)(2,1)S(1)}, bf16[13,64,128]{2,1,0:T(8,128)(2,1)S(1)}, u32[]{:S(2)}, u32[]{:S(2)}) collective-permute-start(bf16[13,64,128]{2,1,0:T(8,128)(2,1)S(1)} %get-tuple-element.19), channel_id=1, source_target_pairs={{0,24},{8,0},{16,8},{24,16},{1,25},{9,1},{17,9},{25,17},{2,26},{10... | collective-permute-start | bytes 638984 | tf_op jit(solution)/shard_map/ppermute | solution.py:548
  16.2 0.0 collective-permute-done.7
  16.3 0.0 collective-permute-done.8
  16.3 0.1 collective-permute-start.10
  16.4 0.5 collective-permute-start.9
  17.0 2.8 %collective-permute-done.2.far_prev_ref = f32[4,16,128]{2,1,0:T(8,128)S(1)} collective-permute-done((f32[4,16,128]{2,1,0:T(8,128)S(1)}, f32[4,16,128]{2,1,0:T(8,128)S(1)}, u32[]{:S(2)}, u32[]{:S(2)}) %collective-permute-start.2) | collective-permute-done | bytes 32800 | tf_op jit(solution)/shard_map/ppermute | solution.py:548
  19.8 2.6 %collective-permute-done.prev_ref = bf16[13,64,128]{2,1,0:T(8,128)(2,1)S(1)} collective-permute-done((bf16[13,64,128]{2,1,0:T(8,128)(2,1)S(1)}, bf16[13,64,128]{2,1,0:T(8,128)(2,1)S(1)}, u32[]{:S(2)}, u32[]{:S(2)}) %collective-permute-start) | collective-permute-done | bytes 213024 | tf_op jit(solution)/shard_map/ppermute | solution.py:548
  22.3 2.4 %collective-permute-done.1.next_ref = bf16[13,64,128]{2,1,0:T(8,128)(2,1)S(1)} collective-permute-done((bf16[13,64,128]{2,1,0:T(8,128)(2,1)S(1)}, bf16[13,64,128]{2,1,0:T(8,128)(2,1)S(1)}, u32[]{:S(2)}, u32[]{:S(2)}) %collective-permute-start.1) | collective-permute-done | bytes 213024 | tf_op jit(solution)/shard_map/ppermute | solution.py:548
  24.7 0.0 copy-start.3
  24.8 0.3 shard_map.38
  25.1 0.1 collective-permute-start.3
  25.1 1.7 %collective-permute-start.4 = (bf16[88,16,128]{2,1,0:T(8,128)(2,1)S(1)}, bf16[88,16,128]{2,1,0:T(8,128)(2,1)S(1)}, u32[]{:S(2)}, u32[]{:S(2)}) collective-permute-start(bf16[88,16,128]{2,1,0:T(8,128)(2,1)S(1)} %get-tuple-element.23), channel_id=1, source_target_pairs={{0,6},{2,0},{4,2},{6,4},{1,7},{3,1},{5,3},{7,5},{8,14},{10,8},{12,... | collective-permute-start | bytes 1081352 | tf_op jit(solution)/shard_map/ppermute | solution.py:548
  26.9 1.5 %collective-permute-start.5 = (f32[8,16,128]{2,1,0:T(8,128)S(1)}, f32[8,16,128]{2,1,0:T(8,128)S(1)}, u32[]{:S(2)}, u32[]{:S(2)}) collective-permute-start(f32[8,16,128]{2,1,0:T(8,128)S(1)} %get-tuple-element.24), channel_id=1, source_target_pairs={{0,4},{2,6},{4,0},{6,2},{1,5},{3,7},{5,1},{7,3},{8,12},{10,14},{12... | collective-permute-start | bytes 196616 | tf_op jit(solution)/shard_map/ppermute | solution.py:548
  28.4 0.0 collective-permute-done.10
  28.4 0.0 collective-permute-done.9
  28.4 0.0 copy-done.1
  28.4 0.2 pad_maximum_fusion.wide_ref
  28.5 0.0 copy-start.4
  28.5 0.6 shard_map.41
  29.1 1.5 %collective-permute-start.11 = (bf16[16,6400]{1,0:T(8,128)(2,1)S(1)}, bf16[16,6400]{1,0:T(8,128)(2,1)S(1)}, u32[]{:S(2)}, u32[]{:S(2)}) collective-permute-start(bf16[16,6400]{1,0:T(8,128)(2,1)S(1)} %shard_map.41), channel_id=1, source_target_pairs={{0,1},{1,0},{2,3},{3,2},{4,5},{5,4},{6,7},{7,6},{8,9},{9,8},{10,11... | collective-permute-start | bytes 614408 | tf_op jit(solution)/shard_map/ppermute | solution.py:548
  30.7 6.5 %collective-permute-done.5.far_prev_ref = f32[8,16,128]{2,1,0:T(8,128)S(1)} collective-permute-done((f32[8,16,128]{2,1,0:T(8,128)S(1)}, f32[8,16,128]{2,1,0:T(8,128)S(1)}, u32[]{:S(2)}, u32[]{:S(2)}) %collective-permute-start.5) | collective-permute-done | bytes 65568 | tf_op jit(solution)/shard_map/ppermute | solution.py:548
  37.2 0.0 collective-permute-done.3.prev_ref
  37.2 0.0 collective-permute-done.4.next_ref
  37.2 0.0 copy-done.3
  37.2 1.0 %shard_map.39 = (f32[6144,128]{1,0:T(8,128)S(1)}, bf16[32,8960]{1,0:T(8,128)(2,1)S(1)}) custom-call(f32[3392,128]{1,0:T(8,128)S(1)} %get-tuple-element.21.x_ref, bf16[88,16,128]{2,1,0:T(8,128)(2,1)S(1)} %collective-permute-done.3.prev_ref, bf16[88,16,128]{2,1,0:T(8,128)(2,1)S(1)} %collective-permute-done.4.next_ref, ...), custom_call_target="tpu_custom_call" | custom-call | flops 67108864 | bytes 1048576 | tf_op jit(solution)/shard_map/pallas_call | solution.py:531
  38.3 1.6 %collective-permute-start.6 = (bf16[32,8960]{1,0:T(8,128)(2,1)S(1)}, bf16[32,8960]{1,0:T(8,128)(2,1)S(1)}, u32[]{:S(2)}, u32[]{:S(2)}) collective-permute-start(bf16[32,8960]{1,0:T(8,128)(2,1)S(1)} %get-tuple-element.26), channel_id=1, source_target_pairs={{0,1},{1,0},{2,3},{3,2},{4,5},{5,4},{6,7},{7,6},{8,9},{9,8},{10,11... | collective-permute-start | bytes 1720328 | tf_op jit(solution)/shard_map/ppermute | solution.py:548
  39.8 0.0 copy-done.4
  39.8 3.9 %shard_map.40 = (bf16[16,128,256]{2,1,0:T(8,128)(2,1)S(1)}, bf16[640,512]{1,0:T(8,128)(2,1)S(1)}) custom-call(f32[16,17]{1,0:T(8,128)S(1)} %bitcast.1), custom_call_target="tpu_custom_call" | custom-call | flops 67108864 | bytes 1048576 | tf_op jit(solution)/shard_map/pallas_call | solution.py:531
  43.8 0.0 collective-permute-done.11.halo_ref
  43.8 8.9 %shard_map.42.fine_ref = f32[64,64,128]{2,1,0:T(8,128)S(1)} custom-call(bf16[80,80,128]{2,1,0:T(8,128)(2,1)S(1)} %pad_maximum_fusion.wide_ref, bf16[16,6400]{1,0:T(8,128)(2,1)S(1)} %collective-permute-done.11.halo_ref, bf16[640,512]{1,0:T(8,128)(2,1)S(1)} %get-tuple-element.27.lanes_ref, bf16[16,128,256]{2,1,0:T(8,128)(2,1)S(1)} %get-tuple-element.28.band_ref), custom_call_target="tpu_custom_call" | custom-call | flops 4294967296 | bytes 1048576 | tf_op jit(solution)/shard_map/pallas_call | solution.py:531
  52.7 0.0 collective-permute-done.6.slab_ref
  52.7 14.6 %shard_map.43 = bf16[64,64,128]{2,1,0:T(8,128)(2,1)} custom-call(f32[6144,128]{1,0:T(8,128)S(1)} %get-tuple-element.25.flat_ref, bf16[32,8960]{1,0:T(8,128)(2,1)S(1)} %collective-permute-done.6.slab_ref, bf16[640,512]{1,0:T(8,128)(2,1)S(1)} %get-tuple-element.27.lanes_ref, bf16[16,128,256]{2,1,0:T(8,128)(2,1)S(1)} %get-tuple-element.28.band_ref, ...), custom_call_target="tpu_custom_call" | custom-call | flops 2147483648 | bytes 1048576 | tf_op jit(solution)/shard_map/pallas_call | solution.py:531
  (5 shorter events, 0.1 us)
Async XLA Ops:
  1.0 15.3 %collective-permute-start.7 = (bf16[8,64,128]{2,1,0:T(8,128)(2,1)S(1)}, bf16[8,64,128]{2,1,0:T(8,128)(2,1)S(1)}, u32[]{:S(2)}, u32[]{:S(2)}) collective-permute-start(bf16[8,64,128]{2,1,0:T(8,128)(2,1)S(1)} %get-tuple-element.31), channel_id=1, source_target_pairs={{0,8},{8,16},{16,24},{24,0},{1,9},{9,17},{17,25},{25,1},{2,10},{10... | collective-permute-start | bytes 393224 | tf_op jit(solution)/shard_map/ppermute | solution.py:548
  4.1 12.2 %collective-permute-start.8 = (bf16[8,64,128]{2,1,0:T(8,128)(2,1)S(1)}, bf16[8,64,128]{2,1,0:T(8,128)(2,1)S(1)}, u32[]{:S(2)}, u32[]{:S(2)}) collective-permute-start(bf16[8,64,128]{2,1,0:T(8,128)(2,1)S(1)} %get-tuple-element.32), channel_id=1, source_target_pairs={{0,24},{8,0},{16,8},{24,16},{1,25},{9,1},{17,9},{25,17},{2,26},{10... | collective-permute-start | bytes 393224 | tf_op jit(solution)/shard_map/ppermute | solution.py:548
  6.2 1.2 %copy-start = (bf16[64,64,128]{2,1,0:T(8,128)(2,1)S(1)}, bf16[64,64,128]{2,1,0:T(8,128)(2,1)}, u32[]{:S(2)}) copy-start(bf16[64,64,128]{2,1,0:T(8,128)(2,1)} %charges_ref.1) | copy-start | bytes 3145732
  7.4 1.0 %copy-start.2 = (bf16[2032,128]{1,0:T(8,128)(2,1)S(1)}, bf16[2032,128]{1,0:T(8,128)(2,1)}, u32[]{:S(2)}) copy-start(bf16[2032,128]{1,0:T(8,128)(2,1)} %constant.2.clone.table_ref.refs_0_) | copy-start | bytes 1560580
  8.5 19.9 %copy-start.1 = (bf16[64,64,128]{2,1,0:T(8,128)(2,1)S(1)}, bf16[64,64,128]{2,1,0:T(8,128)(2,1)}, u32[]{:S(2)}) copy-start(bf16[64,64,128]{2,1,0:T(8,128)(2,1)} %charges_ref.1) | copy-start | bytes 3145732
  11.4 8.3 %collective-permute-start.2 = (f32[4,16,128]{2,1,0:T(8,128)S(1)}, f32[4,16,128]{2,1,0:T(8,128)S(1)}, u32[]{:S(2)}, u32[]{:S(2)}) collective-permute-start(f32[4,16,128]{2,1,0:T(8,128)S(1)} %get-tuple-element.20), channel_id=1, source_target_pairs={{0,16},{8,24},{16,0},{24,8},{1,17},{9,25},{17,1},{25,9},{2,18},{10... | collective-permute-start | bytes 98312 | tf_op jit(solution)/shard_map/ppermute | solution.py:548
  12.4 9.9 %collective-permute-start = (bf16[13,64,128]{2,1,0:T(8,128)(2,1)S(1)}, bf16[13,64,128]{2,1,0:T(8,128)(2,1)S(1)}, u32[]{:S(2)}, u32[]{:S(2)}) collective-permute-start(bf16[13,64,128]{2,1,0:T(8,128)(2,1)S(1)} %get-tuple-element.18), channel_id=1, source_target_pairs={{0,8},{8,16},{16,24},{24,0},{1,9},{9,17},{17,25},{25,1},{2,10},{10... | collective-permute-start | bytes 638984 | tf_op jit(solution)/shard_map/ppermute | solution.py:548
  14.0 10.8 %collective-permute-start.1 = (bf16[13,64,128]{2,1,0:T(8,128)(2,1)S(1)}, bf16[13,64,128]{2,1,0:T(8,128)(2,1)S(1)}, u32[]{:S(2)}, u32[]{:S(2)}) collective-permute-start(bf16[13,64,128]{2,1,0:T(8,128)(2,1)S(1)} %get-tuple-element.19), channel_id=1, source_target_pairs={{0,24},{8,0},{16,8},{24,16},{1,25},{9,1},{17,9},{25,17},{2,26},{10... | collective-permute-start | bytes 638984 | tf_op jit(solution)/shard_map/ppermute | solution.py:548
  16.3 12.0 %collective-permute-start.10 = (bf16[80,8,128]{2,1,0:T(8,128)(2,1)S(1)}, bf16[80,8,128]{2,1,0:T(8,128)(2,1)S(1)}, u32[]{:S(2)}, u32[]{:S(2)}) collective-permute-start(bf16[80,8,128]{2,1,0:T(8,128)(2,1)S(1)} %pad_maximum_fusion.2), channel_id=1, source_target_pairs={{0,6},{2,0},{4,2},{6,4},{1,7},{3,1},{5,3},{7,5},{8,14},{10,8},{12,... | collective-permute-start | bytes 491528 | tf_op jit(solution)/shard_map/ppermute | solution.py:548
  16.4 11.9 %collective-permute-start.9 = (bf16[80,8,128]{2,1,0:T(8,128)(2,1)S(1)}, bf16[80,8,128]{2,1,0:T(8,128)(2,1)S(1)}, u32[]{:S(2)}, u32[]{:S(2)}) collective-permute-start(bf16[80,8,128]{2,1,0:T(8,128)(2,1)S(1)} %pad_maximum_fusion.1), channel_id=1, source_target_pairs={{0,2},{2,4},{4,6},{6,0},{1,3},{3,5},{5,7},{7,1},{8,10},{10,12},{12... | collective-permute-start | bytes 491528 | tf_op jit(solution)/shard_map/ppermute | solution.py:548
  24.7 12.5 %copy-start.3 = (bf16[2032,128]{1,0:T(8,128)(2,1)S(1)}, bf16[2032,128]{1,0:T(8,128)(2,1)}, u32[]{:S(2)}) copy-start(bf16[2032,128]{1,0:T(8,128)(2,1)} %constant.2.clone.table_ref.refs_0_) | copy-start | bytes 1560580
  25.1 12.2 %collective-permute-start.3 = (bf16[88,16,128]{2,1,0:T(8,128)(2,1)S(1)}, bf16[88,16,128]{2,1,0:T(8,128)(2,1)S(1)}, u32[]{:S(2)}, u32[]{:S(2)}) collective-permute-start(bf16[88,16,128]{2,1,0:T(8,128)(2,1)S(1)} %get-tuple-element.22), channel_id=1, source_target_pairs={{0,2},{2,4},{4,6},{6,0},{1,3},{3,5},{5,7},{7,1},{8,10},{10,12},{12... | collective-permute-start | bytes 1081352 | tf_op jit(solution)/shard_map/ppermute | solution.py:548
  25.1 12.1 %collective-permute-start.4 = (bf16[88,16,128]{2,1,0:T(8,128)(2,1)S(1)}, bf16[88,16,128]{2,1,0:T(8,128)(2,1)S(1)}, u32[]{:S(2)}, u32[]{:S(2)}) collective-permute-start(bf16[88,16,128]{2,1,0:T(8,128)(2,1)S(1)} %get-tuple-element.23), channel_id=1, source_target_pairs={{0,6},{2,0},{4,2},{6,4},{1,7},{3,1},{5,3},{7,5},{8,14},{10,8},{12,... | collective-permute-start | bytes 1081352 | tf_op jit(solution)/shard_map/ppermute | solution.py:548
  26.9 10.4 %collective-permute-start.5 = (f32[8,16,128]{2,1,0:T(8,128)S(1)}, f32[8,16,128]{2,1,0:T(8,128)S(1)}, u32[]{:S(2)}, u32[]{:S(2)}) collective-permute-start(f32[8,16,128]{2,1,0:T(8,128)S(1)} %get-tuple-element.24), channel_id=1, source_target_pairs={{0,4},{2,6},{4,0},{6,2},{1,5},{3,7},{5,1},{7,3},{8,12},{10,14},{12... | collective-permute-start | bytes 196616 | tf_op jit(solution)/shard_map/ppermute | solution.py:548
  28.5 11.3 %copy-start.4 = (f32[4,4,17]{2,1,0:T(4,128)S(1)}, f32[4,4,17]{2,1,0:T(4,128)}, u32[]{:S(2)}) copy-start(f32[4,4,17]{2,1,0:T(4,128)} %param.4) | copy-start | bytes 3268
  29.1 14.6 %collective-permute-start.11 = (bf16[16,6400]{1,0:T(8,128)(2,1)S(1)}, bf16[16,6400]{1,0:T(8,128)(2,1)S(1)}, u32[]{:S(2)}, u32[]{:S(2)}) collective-permute-start(bf16[16,6400]{1,0:T(8,128)(2,1)S(1)} %shard_map.41), channel_id=1, source_target_pairs={{0,1},{1,0},{2,3},{3,2},{4,5},{5,4},{6,7},{7,6},{8,9},{9,8},{10,11... | collective-permute-start | bytes 614408 | tf_op jit(solution)/shard_map/ppermute | solution.py:548
  38.3 14.4 %collective-permute-start.6 = (bf16[32,8960]{1,0:T(8,128)(2,1)S(1)}, bf16[32,8960]{1,0:T(8,128)(2,1)S(1)}, u32[]{:S(2)}, u32[]{:S(2)}) collective-permute-start(bf16[32,8960]{1,0:T(8,128)(2,1)S(1)} %get-tuple-element.26), channel_id=1, source_target_pairs={{0,1},{1,0},{2,3},{3,2},{4,5},{5,4},{6,7},{7,6},{8,9},{9,8},{10,11... | collective-permute-start | bytes 1720328 | tf_op jit(solution)/shard_map/ppermute | solution.py:548
where the time goes:
time: 67.6 us; the launch traced here: 67.4 us
  Pallas kernels  32.4 us (48%)
  starting transfers between devices  17 us (25%)
  waiting for transfers between devices  14.3 us (21%)
  local copies, waits for them, and re-layouts  3.31 us (5%)
    pallas_call x7, Pallas kernels, call(): pl.pallas_call(kernel, out_shape=out_shape, in_specs=specs, out_specs=out...  32.4 us
    ppermute x12, starting transfers between devices, shifted(): lax.ppermute(value, axis, [(i, (i + by) % count) for i in range(count)])  17 us
    ppermute x12, waiting for transfers between devices, shifted(): lax.ppermute(value, axis, [(i, (i + by) % count) for i in range(count)])  14.3 us
    unnamed x10, local copies, waits for them, and re-layouts  2.28 us
  transfers between devices with their start and end apart: 12, of which 4 were waited for; matrix products, arithmetic and copies ran while one was open for 0% of the time, Pallas kernels for 26%

commit v1 on v0

--- a/solution.py
+++ b/solution.py
@@ -7,6 +7,7 @@
 from jax.experimental import pallas as pl
 from jax.experimental.pallas import tpu as pltpu
 from jax.sharding import PartitionSpec as P
+
 
 F32, BF16 = jnp.float32, jnp.bfloat16
 REACH = 8
@@ -52,26 +53,31 @@
     return (level.lane + z + level.low + REACH) % LANES
 
 
+def stencil_of(offset, valid):
+    size = jnp.abs(offset)
+    weight = jnp.where(size == 0, 1.0, jnp.where(size == 1, 9 / 16, jnp.where(size == 3, -1 / 16, 0.0)))
+    return jnp.where(valid, weight, 0.0).astype(BF16)
+
+
 def restrict_rows(coarse, fine):
     fine_rows = fine.n[1] if fine.index == 0 else fine.rows
-    matrix = np.zeros((coarse.rows, 2, fine_rows))
-    for row in range(coarse.win[1]):
-        for offset, weight in STENCIL:
-            col = 2 * (row - coarse.low) + offset + fine.low
-            if 0 <= col < fine.win[1]:
-                matrix[row, :, col] = weight
-    return matrix.reshape(coarse.rows, 2 * fine_rows)
+    row = lax.broadcasted_iota(jnp.int32, (coarse.rows, 2 * fine_rows), 0)
+    col = lax.broadcasted_iota(jnp.int32, (coarse.rows, 2 * fine_rows), 1)
+    col = jnp.where(col >= fine_rows, col - fine_rows, col)
+    valid = (row < coarse.win[1]) & (col < fine.win[1])
+    return stencil_of(col - fine.low - 2 * (row - coarse.low), valid)
 
 
 def restrict_lanes(coarse, fine):
-    matrix = np.zeros((2, LANES, LANES))
-    for z in range(-coarse.low, coarse.n[2] + coarse.high):
-        for offset, weight in STENCIL:
-            at = 2 * z + offset
-            if -fine.low <= at < fine.n[2] + fine.high:
-                lane = at if fine.index == 0 else own_lane(fine, at)
-                matrix[:, lane, own_lane(coarse, z)] = weight
-    return matrix.reshape(2 * LANES, LANES)
+    k = lax.broadcasted_iota(jnp.int32, (2 * LANES, LANES), 0) % LANES
+    lane = lax.broadcasted_iota(jnp.int32, (2 * LANES, LANES), 1)
+
+    def place(level, lanes):
+        return lanes if level.index == 0 else (lanes + (2 * LANES - level.lane - REACH)) % LANES
+
+    k, lane = place(fine, k), place(coarse, lane)
+    valid = (k < fine.win[2]) & (lane < coarse.win[2])
+    return stencil_of(k - fine.low - 2 * (lane - coarse.low), valid)
 
 
 def prolong_weights(fine_at):
@@ -220,8 +226,11 @@
     return high, x - high
 
 
-def restrict_kernel(levels, table, charges_ref, table_ref, q_ref, up_ref, down_ref, far_ref):
+def restrict_kernel(
+    levels, charges_ref, q_ref, up_ref, down_ref, far_ref
+):
     for level, fine in zip(levels[1:], levels[:3]):
+        by_rows, by_lanes = restrict_rows(level, fine), restrict_lanes(level, fine)
         for at in range(level.win[0]):
             terms = {}
             for offset, weight in STENCIL:
@@ -233,38 +242,71 @@
                         value = q_ref[plane_at(levels, fine, plane, "own")]
                     terms.setdefault(weight, []).append(value)
             value = total([total(group) * weight for weight, group in terms.items()])
-            value = dot(table.get(table_ref, "rows", level.index), split_rows(value))
-            value = dot(split_lanes(value), table.get(table_ref, "lanes", level.index))
+            value = dot(by_rows, split_rows(value))
+            value = dot(split_lanes(value), by_lanes)
             q_ref[plane_at(levels, level, at, "own")] = value
-    rows, rest_rows = levels[1].rows, levels[2].rows
-    for j in range(up_ref.shape[0]):
+    high_rows, rest_rows = levels[1].rows, levels[2].rows
+    pitch = slab_pitch(levels)
+    planes = slab_planes(levels)
+    for j in range(planes):
         for slab_ref, bases in ((up_ref, [lv.n[0] - REACH for lv in levels[1:]]), (down_ref, [0] * 3)):
             highs, rests = [], [jnp.zeros((rest_rows, LANES), F32)]
             for level, base in zip(levels[1:], bases):
                 if base + j < level.win[0]:
                     high, rest = halves_of(q_ref[plane_at(levels, level, base + j, "own")])
-                    highs.append(pad_rows(high, rows))
+                    highs.append(pad_rows(high, high_rows))
                     if level.index > 1:
                         rests.append(pad_rows(rest, rest_rows))
-            slab_ref[j] = jnp.concatenate([total(highs), total(rests)], 0).astype(BF16)
+            rest = jnp.concatenate([jnp.zeros((rest_rows, LANES), F32), total(rests)], 0)
+            value = pad_rows(total(highs), pitch) + rest
+            slab_ref[j * pitch : (j + 1) * pitch] = value.astype(BF16)
     last = levels[3]
     pack_far(
+        levels,
         far_ref,
         [q_ref[plane_at(levels, last, at, "own")] for at in range(last.win[0])],
     )
 
 
-def pack_far(far_ref, planes):
+def slab_planes(levels):
+    return max(level.low + level.high + REACH for level in levels[1:])
+
+
+def slab_pitch(levels):
+    return up_to(max(levels[1].rows, 2 * levels[2].rows), TILE)
+
+
+def rest_block(levels, plane):
+    spare = levels[1].full[0] - levels[2].full[0]
+    if plane < spare:
+        return levels[2].full[0] + plane, 0
+    return levels[1].full[0] + (plane - spare) // 2, LANES // 2 * ((plane - spare) % 2)
+
+
+def slab_blocks(levels):
+    return rest_block(levels, levels[2].full[0] - 1)[0] + 1
+
+
+def turned(x, lanes):
+    return pltpu.roll(x, lanes % LANES, 1) if lanes % LANES else x
+
+
+def far_groups(levels, planes):
+    return -(-planes // (LANES // levels[3].win[2]))
+
+
+def pack_far(levels, far_ref, planes):
+    width = levels[3].win[2]
+    per = LANES // width
     for group in range(far_ref.shape[0]):
-        members = planes[4 * group : 4 * group + 4]
-        far_ref[group] = total(
-            [pltpu.roll(x, 32 * k, 1) if k else x for k, x in enumerate(members)]
-        )
-
-
-def unpack_far(far_ref, at):
-    x = far_ref[at // 4]
-    return pltpu.roll(x, LANES - 32 * (at % 4), 1) if at % 4 else x
+        members = planes[per * group : per * group + per]
+        far_ref[group] = total([turned(x, width * k) for k, x in enumerate(members)])
+
+
+def unpack_far(levels, far_ref, at):
+    width = levels[3].win[2]
+    per = LANES // width
+    return turned(far_ref[at // per], LANES - width * (at % per))
 
 
 def lane_masks(levels):
@@ -279,18 +321,17 @@
 def rows_kernel(levels, q_ref, prev_ref, next_ref, far_prev_ref, *refs):
     far_next_ref = far_prev_ref if len(refs) == 4 else refs[0]
     x_ref, up_ref, down_ref, far_ref = refs[-4:]
-    count, high_rows = prev_ref.shape[0], levels[1].rows
+    count, pitch, rest_rows = slab_planes(levels), slab_pitch(levels), levels[2].rows
     masks = lane_masks(levels)
     coarsest = []
 
     def received(ref, at, level):
-        slab = ref[at].astype(F32)
+        slab = ref[at * pitch : (at + 1) * pitch].astype(F32)
         high = slab[: level.rows]
-        return high if level.index == 1 else high + slab[high_rows : high_rows + level.rows]
-
-    rest_count = levels[2].full[0]
+        return high if level.index == 1 else high + slab[rest_rows : rest_rows + level.rows]
+
+    blocks = {True: {}, False: {}}
     for at in range(levels[1].full[0]):
-        ups, downs = [], []
         for level, mask in zip(levels[1:], masks):
             if at >= level.full[0]:
                 continue
@@ -304,31 +345,39 @@
                 terms.append(received(next_ref, at - REACH - n, level))
             if level.index == 3:
                 if at - REACH + 2 * n < level.win[0]:
-                    terms.append(unpack_far(far_prev_ref, at - REACH + 2 * n))
+                    terms.append(unpack_far(levels, far_prev_ref, at - REACH + 2 * n))
                 if at - REACH - 2 * n >= 0:
-                    terms.append(unpack_far(far_next_ref, at - REACH - 2 * n))
+                    terms.append(unpack_far(levels, far_next_ref, at - REACH - 2 * n))
             value = jnp.where(mask, total(terms), 0.0)
             x_ref[plane_at(levels, level, at, "full")] = value
             first = level.n[1] - REACH
-            ups.append((level.index, halves_of(value[first : first + SLAB])))
-            downs.append((level.index, halves_of(value[:SLAB])))
+            for is_up, rows in ((True, value[first : first + SLAB]), (False, value[:SLAB])):
+                high, rest = halves_of(rows)
+                blocks[is_up].setdefault(at, []).append(high)
+                if level.index > 1:
+                    block, lanes = rest_block(levels, at)
+                    blocks[is_up].setdefault(block, []).append(turned(rest, lanes))
             if level.index == 3:
                 coarsest.append(value)
-        for slab_ref, parts in ((up_ref, ups), (down_ref, downs)):
-            slab_ref[at] = total([x for _, (x, _) in parts]).astype(BF16)
-            rests = [x for index, (_, x) in parts if index > 1]
-            if rests:
-                slab_ref[levels[1].full[0] + at] = total(rests).astype(BF16)
-    pack_far(far_ref, coarsest)
+    for is_up, slab_ref in ((True, up_ref), (False, down_ref)):
+        for block, parts in blocks[is_up].items():
+            slab_ref[block * SLAB : (block + 1) * SLAB] = total(parts).astype(BF16)
+    pack_far(levels, far_ref, coarsest)
 
 
 def lanes_kernel(levels, table, x_ref, prev_ref, next_ref, far_prev_ref, *refs):
     far_next_ref = far_prev_ref if len(refs) == 3 else refs[0]
     table_ref, flat_ref, slab_ref = refs[-3:]
 
+    def block_of(ref, block):
+        return ref[block * SLAB : (block + 1) * SLAB].astype(F32)
+
     def received(ref, at, level):
-        high = ref[at].astype(F32)
-        return high if level.index == 1 else high + ref[levels[1].full[0] + at].astype(F32)
+        high = block_of(ref, at)
+        if level.index == 1:
+            return high
+        block, lanes = rest_block(levels, at)
+        return high + turned(block_of(ref, block), LANES - lanes)
 
     for level, mask in zip(levels[1:], lane_masks(levels)):
         blocks, step = level.inp[1] // 8, level.n[1] // 8
@@ -336,7 +385,7 @@
             own = x_ref[plane_at(levels, level, at, "full")]
             slabs = [received(prev_ref, at, level), received(next_ref, at, level)]
             if level.index == 3:
-                slabs += [unpack_far(far_prev_ref, at), unpack_far(far_next_ref, at)]
+                slabs += [unpack_far(levels, ref, at) for ref in (far_prev_ref, far_next_ref)]
             parts = []
             for block in range(blocks):
                 terms = []
@@ -512,8 +561,6 @@
 def make_table(levels):
     table = Table()
     for level, fine in zip(levels[1:], levels[:3]):
-        table.add(("rows", level.index), restrict_rows(level, fine))
-        table.add(("lanes", level.index), restrict_lanes(level, fine))
         table.add(("send", level.index), send_lanes(level))
         table.add(("place", level.index), place_lanes(level))
         table.add(("tall", fine.index), prolong_rows(fine, level))
@@ -521,10 +568,13 @@
     return table
 
 
-def call(kernel, out_shape, args, scratch=(), smem=(), flops=0, limit=12):
-    specs = [
-        pl.BlockSpec(memory_space=pltpu.SMEM if i in smem else pltpu.VMEM) for i in range(len(args))
-    ]
+def ends_kernel(charges_ref, last_ref, first_ref):
+    last_ref[...] = charges_ref[charges_ref.shape[0] - REACH :]
+    first_ref[...] = charges_ref[:REACH]
+
+
+def call(kernel, out_shape, args, scratch=(), spaces={}, flops=0, limit=12):
+    specs = [pl.BlockSpec(memory_space=spaces.get(i, pltpu.VMEM)) for i in range(len(args))]
     single = not isinstance(out_shape, (list, tuple))
     outs = [out_shape] if single else list(out_shape)
     out_specs = [pl.BlockSpec(memory_space=pltpu.VMEM) for _ in outs]
@@ -560,53 +610,60 @@
     return jnp.concatenate([shifted(value[:half], axis, 1), shifted(value[half:], axis, -1)], 0)
 
 
-def per_device(charges, taps):
+def steps(charges, taps):
     levels = levels_of(charges.shape)
     table = make_table(levels)
     table_array = table.array()
     zero, coarse = levels[0], levels[1:]
     reach = REACH
 
-    x_prev = shifted(charges[-reach:], "gx", 1)
-    x_next = shifted(charges[:reach], "gx", -1)
-
-    slab_planes = max(level.low + level.high + reach for level in coarse)
-    slab_rows = levels[1].rows + levels[2].rows
-    q, l_up, l_down, l_far = call(
-        functools.partial(restrict_kernel, levels, table),
-        [shape((sum(lv.win[0] * lv.rows for lv in coarse), LANES), F32)]
-        + [shape((slab_planes, slab_rows, LANES), BF16)] * 2
-        + [shape((up_to(levels[3].win[0], 4) // 4, SLAB, LANES), F32)],
-        [charges, table_array],
+    last, first = call(
+        ends_kernel, [shape((reach, *charges.shape[1:]), BF16)] * 2, [charges], flops=1 << 20
+    )
+    x_prev = shifted(last, "gx", 1)
+    x_next = shifted(first, "gx", -1)
+
+    x_slab = shape((slab_planes(levels) * slab_pitch(levels), LANES), BF16)
+    q, up, down, far = call(
+        functools.partial(restrict_kernel, levels),
+        [
+            shape((sum(lv.win[0] * lv.rows for lv in coarse), LANES), F32),
+            x_slab,
+            x_slab,
+            shape((far_groups(levels, levels[3].win[0]), SLAB, LANES), F32),
+        ],
+        [charges],
         flops=1 << 27,
     )
     band, lanes = call(
         functools.partial(bands_kernel, levels),
         [shape((16, 8 * TILE, 16 * TILE), BF16), shape((5 * LANES, 4 * LANES), BF16)],
         [taps.reshape(16, 17)],
-        smem=(0,),
+        spaces={0: pltpu.SMEM},
         flops=1 << 26,
     )
-
-    l_prev = shifted(l_up, "gx", 1)
-    l_next = shifted(l_down, "gx", -1)
-    far = far_pair(l_far, "gx")
-
+    from_prev = shifted(up, "gx", 1)
+    from_next = shifted(down, "gx", -1)
+    far = far_pair(far, "gx")
     pieces = (x_prev, charges, x_next)
     y_prev = shifted(jnp.concatenate([x[:, -reach:] for x in pieces], 0), "gy", 1)
     y_next = shifted(jnp.concatenate([x[:, :reach] for x in pieces], 0), "gy", -1)
 
-    r, m_up, m_down, m_far = call(
+    y_slab = shape((slab_blocks(levels) * SLAB, LANES), BF16)
+    r, up, down, far = call(
         functools.partial(rows_kernel, levels),
-        [shape((sum(lv.full[0] * lv.rows for lv in coarse), LANES), F32)]
-        + [shape((levels[1].full[0] + levels[2].full[0], SLAB, LANES), BF16)] * 2
-        + [shape((up_to(levels[3].full[0], 4) // 4, SLAB, LANES), F32)],
-        [q, l_prev, l_next, *far],
+        [
+            shape((sum(lv.full[0] * lv.rows for lv in coarse), LANES), F32),
+            y_slab,
+            y_slab,
+            shape((far_groups(levels, levels[3].full[0]), SLAB, LANES), F32),
+        ],
+        [q, from_prev, from_next, *far],
         flops=1 << 25,
     )
-    m_prev = shifted(m_up, "gy", 1)
-    m_next = shifted(m_down, "gy", -1)
-    far = far_pair(m_far, "gy")
+    m_prev = shifted(up, "gy", 1)
+    m_next = shifted(down, "gy", -1)
+    far = far_pair(far, "gy")
 
     wide = jnp.concatenate([y_prev, jnp.concatenate(pieces, 0), y_next], 1)
     sides = call(
@@ -654,7 +711,7 @@
 
 def solution(mesh):
     return jax.shard_map(
-        per_device,
+        steps,
         mesh=mesh,
         in_specs=(P("gx", "gy", "gz"), P()),
         out_specs=P("gx", "gy", "gz"),

time: 67.6 us -> 60.5 us (0.89)
  waiting for transfers between devices: 14.3 us -> 10.3 us
  local copies, waits for them, and re-layouts: 3.31 us -> 1.29 us
  starting transfers between devices: 17 us -> 16.1 us
    ppermute x12, waiting for transfers between devices: 14.3 us -> 10.3 us  [shifted(): lax.ppermute(value, axis, [(i, (i + by) % count) for i in range(count)])]
    unnamed x10 -> x8, local copies, waits for them, and re-layouts: 2.28 us -> 1.24 us
    slice x4 -> x3, local copies, waits for them, and re-layouts: 1.04 us -> 0.05 us  [steps(): x[:, -reach:]]
    ppermute x12, starting transfers between devices: 17 us -> 16.1 us  [shifted(): lax.ppermute(value, axis, [(i, (i + by) % count) for i in range(count)])]
    pallas_call x7 -> x8, Pallas kernels: 32.4 us -> 32.4 us  [call(): pl.pallas_call(kernel, out_shape=out_shape, in_specs=specs, out_specs=out...]
  transfers between devices with their start and end apart: 12 -> 12, of which waited for: 4 -> 3; matrix products, arithmetic and copies ran while one was open for 0% -> 0% of each run, Pallas kernels for 26% -> 29%
where the time goes in v1:
time: 60.5 us; the launch traced here: 60.4 us
  Pallas kernels  32.4 us (54%)
  starting transfers between devices  16.1 us (27%)
  waiting for transfers between devices  10.3 us (17%)
  local copies, waits for them, and re-layouts  1.29 us (2%)
    pallas_call x8, Pallas kernels, call(): pl.pallas_call(kernel, out_shape=out_shape, in_specs=specs, out_specs=out...  32.4 us
    ppermute x12, starting transfers between devices, shifted(): lax.ppermute(value, axis, [(i, (i + by) % count) for i in range(count)])  16.1 us
    ppermute x12, waiting for transfers between devices, shifted(): lax.ppermute(value, axis, [(i, (i + by) % count) for i in range(count)])  10.3 us
    unnamed x8, local copies, waits for them, and re-layouts  1.24 us
  transfers between devices with their start and end apart: 12, of which 3 were waited for; matrix products, arithmetic and copies ran while one was open for 0% of the time, Pallas kernels for 29%

profile of v1, /device:TPU:0, one launch (start us, length us, event | category | flops | bytes accessed | tf_op | source)
XLA Modules:
  0.0 60.4 jit_solution(8208665145178795800)
XLA Ops:
  0.0 0.0 copy-start
  0.0 1.2 %copy-done = bf16[64,64,128]{2,1,0:T(8,128)(2,1)S(1)} copy-done((bf16[64,64,128]{2,1,0:T(8,128)(2,1)S(1)}, bf16[64,64,128]{2,1,0:T(8,128)(2,1)}, u32[]{:S(2)}) %copy-start) | copy-done | bytes 1048600
  1.2 0.0 copy-start.1
  1.2 3.1 %collective-permute-start.7 = (bf16[8,64,128]{2,1,0:T(8,128)(2,1)S(1)}, bf16[8,64,128]{2,1,0:T(8,128)(2,1)S(1)}, u32[]{:S(2)}, u32[]{:S(2)}) collective-permute-start(bf16[8,64,128]{2,1,0:T(8,128)(2,1)S(1)} %get-tuple-element.31), channel_id=1, source_target_pairs={{0,8},{8,16},{16,24},{24,0},{1,9},{9,17},{17,25},{25,1},{2,10},{10... | collective-permute-start | bytes 393224 | tf_op jit(solution)/shard_map/ppermute | solution.py:598
  4.4 2.1 %collective-permute-start.8 = (bf16[8,64,128]{2,1,0:T(8,128)(2,1)S(1)}, bf16[8,64,128]{2,1,0:T(8,128)(2,1)S(1)}, u32[]{:S(2)}, u32[]{:S(2)}) collective-permute-start(bf16[8,64,128]{2,1,0:T(8,128)(2,1)S(1)} %get-tuple-element.32), channel_id=1, source_target_pairs={{0,24},{8,0},{16,8},{24,16},{1,25},{9,1},{17,9},{25,17},{2,26},{10... | collective-permute-start | bytes 393224 | tf_op jit(solution)/shard_map/ppermute | solution.py:598
  6.4 3.0 %shard_map.37 = (f32[2112,128]{1,0:T(8,128)S(1)}, bf16[624,128]{1,0:T(8,128)(2,1)S(1)}, bf16[624,128]{1,0:T(8,128)(2,1)S(1)}, f32[3,16,128]{2,1,0:T(8,128)S(1)}) custom-call(bf16[64,64,128]{2,1,0:T(8,128)(2,1)S(1)} %copy-done), custom_call_target="tpu_custom_call" | custom-call | flops 134217728 | bytes 1048576 | tf_op jit(solution)/shard_map/pallas_call | solution.py:581
  9.4 0.0 collective-permute-start
  9.5 3.8 %collective-permute-start.1 = (bf16[624,128]{1,0:T(8,128)(2,1)S(1)}, bf16[624,128]{1,0:T(8,128)(2,1)S(1)}, u32[]{:S(2)}, u32[]{:S(2)}) collective-permute-start(bf16[624,128]{1,0:T(8,128)(2,1)S(1)} %get-tuple-element.21), channel_id=1, source_target_pairs={{0,24},{8,0},{16,8},{24,16},{1,25},{9,1},{17,9},{25,17},{2,26},{10... | collective-permute-start | bytes 479240 | tf_op jit(solution)/shard_map/ppermute | solution.py:598
  13.3 0.0 collective-permute-done.7
  13.4 0.0 collective-permute-done.8
  13.4 0.1 collective-permute-start.10
  13.6 0.5 collective-permute-start.9
  14.1 0.0 collective-permute-start.2
  14.1 6.3 %collective-permute-done.2.far_prev_ref = f32[3,16,128]{2,1,0:T(8,128)S(1)} collective-permute-done((f32[3,16,128]{2,1,0:T(8,128)S(1)}, f32[3,16,128]{2,1,0:T(8,128)S(1)}, u32[]{:S(2)}, u32[]{:S(2)}) %collective-permute-start.2) | collective-permute-done | bytes 24608 | tf_op jit(solution)/shard_map/ppermute | solution.py:598
  20.3 0.0 collective-permute-done.prev_ref
  20.3 0.0 collective-permute-done.1.next_ref
  20.3 0.0 copy-start.2
  20.3 0.3 shard_map.38
  20.7 0.1 collective-permute-start.3
  20.7 1.7 %collective-permute-start.4 = (bf16[1008,128]{1,0:T(8,128)(2,1)S(1)}, bf16[1008,128]{1,0:T(8,128)(2,1)S(1)}, u32[]{:S(2)}, u32[]{:S(2)}) collective-permute-start(bf16[1008,128]{1,0:T(8,128)(2,1)S(1)} %get-tuple-element.25), channel_id=1, source_target_pairs={{0,6},{2,0},{4,2},{6,4},{1,7},{3,1},{5,3},{7,5},{8,14},{10,8},{12,... | collective-permute-start | bytes 774152 | tf_op jit(solution)/shard_map/ppermute | solution.py:598
  22.5 0.0 copy-start.3
  22.5 1.5 %collective-permute-start.5 = (f32[5,16,128]{2,1,0:T(8,128)S(1)}, f32[5,16,128]{2,1,0:T(8,128)S(1)}, u32[]{:S(2)}, u32[]{:S(2)}) collective-permute-start(f32[5,16,128]{2,1,0:T(8,128)S(1)} %get-tuple-element.26), channel_id=1, source_target_pairs={{0,4},{2,6},{4,0},{6,2},{1,5},{3,7},{5,1},{7,3},{8,12},{10,14},{12... | collective-permute-start | bytes 122888 | tf_op jit(solution)/shard_map/ppermute | solution.py:598
  24.0 0.0 collective-permute-done.10
  24.0 0.0 collective-permute-done.9
  24.0 0.0 copy-done.1
  24.0 0.2 pad_maximum_fusion.wide_ref
  24.1 0.6 %shard_map.42 = bf16[16,6400]{1,0:T(8,128)(2,1)S(1)} custom-call(bf16[80,80,128]{2,1,0:T(8,128)(2,1)S(1)} %pad_maximum_fusion.wide_ref), custom_call_target="tpu_custom_call" | custom-call | flops 67108864 | bytes 1048576 | tf_op jit(solution)/shard_map/pallas_call | solution.py:581
  24.7 1.5 %collective-permute-start.11 = (bf16[16,6400]{1,0:T(8,128)(2,1)S(1)}, bf16[16,6400]{1,0:T(8,128)(2,1)S(1)}, u32[]{:S(2)}, u32[]{:S(2)}) collective-permute-start(bf16[16,6400]{1,0:T(8,128)(2,1)S(1)} %shard_map.42), channel_id=1, source_target_pairs={{0,1},{1,0},{2,3},{3,2},{4,5},{5,4},{6,7},{7,6},{8,9},{9,8},{10,11... | collective-permute-start | bytes 614408 | tf_op jit(solution)/shard_map/ppermute | solution.py:598
  26.3 3.8 %collective-permute-done.5.far_prev_ref = f32[5,16,128]{2,1,0:T(8,128)S(1)} collective-permute-done((f32[5,16,128]{2,1,0:T(8,128)S(1)}, f32[5,16,128]{2,1,0:T(8,128)S(1)}, u32[]{:S(2)}, u32[]{:S(2)}) %collective-permute-start.5) | collective-permute-done | bytes 40992 | tf_op jit(solution)/shard_map/ppermute | solution.py:598
  30.1 0.0 collective-permute-done.3.prev_ref
  30.1 0.0 collective-permute-done.4.next_ref
  30.1 0.0 copy-done.2
  30.1 1.0 %shard_map.39 = (f32[6144,128]{1,0:T(8,128)S(1)}, bf16[32,8960]{1,0:T(8,128)(2,1)S(1)}) custom-call(f32[3392,128]{1,0:T(8,128)S(1)} %get-tuple-element.23.x_ref, bf16[1008,128]{1,0:T(8,128)(2,1)S(1)} %collective-permute-done.3.prev_ref, bf16[1008,128]{1,0:T(8,128)(2,1)S(1)} %collective-permute-done.4.next_ref, ...), custom_call_target="tpu_custom_call" | custom-call | flops 67108864 | bytes 1048576 | tf_op jit(solution)/shard_map/pallas_call | solution.py:581
  31.1 1.6 %collective-permute-start.6 = (bf16[32,8960]{1,0:T(8,128)(2,1)S(1)}, bf16[32,8960]{1,0:T(8,128)(2,1)S(1)}, u32[]{:S(2)}, u32[]{:S(2)}) collective-permute-start(bf16[32,8960]{1,0:T(8,128)(2,1)S(1)} %get-tuple-element.28), channel_id=1, source_target_pairs={{0,1},{1,0},{2,3},{3,2},{4,5},{5,4},{6,7},{7,6},{8,9},{9,8},{10,11... | collective-permute-start | bytes 1720328 | tf_op jit(solution)/shard_map/ppermute | solution.py:598
  32.7 0.0 copy-done.3
  32.7 3.9 %shard_map.40 = (bf16[16,128,256]{2,1,0:T(8,128)(2,1)S(1)}, bf16[640,512]{1,0:T(8,128)(2,1)S(1)}) custom-call(f32[16,17]{1,0:T(8,128)S(1)} %bitcast.1), custom_call_target="tpu_custom_call" | custom-call | flops 67108864 | bytes 1048576 | tf_op jit(solution)/shard_map/pallas_call | solution.py:581
  36.6 0.0 collective-permute-done.11.halo_ref
  36.7 8.9 %shard_map.43.fine_ref = f32[64,64,128]{2,1,0:T(8,128)S(1)} custom-call(bf16[80,80,128]{2,1,0:T(8,128)(2,1)S(1)} %pad_maximum_fusion.wide_ref, bf16[16,6400]{1,0:T(8,128)(2,1)S(1)} %collective-permute-done.11.halo_ref, bf16[640,512]{1,0:T(8,128)(2,1)S(1)} %get-tuple-element.29.lanes_ref, bf16[16,128,256]{2,1,0:T(8,128)(2,1)S(1)} %get-tuple-element.30.band_ref), custom_call_target="tpu_custom_call" | custom-call | flops 4294967296 | bytes 1048576 | tf_op jit(solution)/shard_map/pallas_call | solution.py:581
  45.6 0.1 collective-permute-done.6.slab_ref
  45.7 14.6 %shard_map.44 = bf16[64,64,128]{2,1,0:T(8,128)(2,1)} custom-call(f32[6144,128]{1,0:T(8,128)S(1)} %get-tuple-element.27.flat_ref, bf16[32,8960]{1,0:T(8,128)(2,1)S(1)} %collective-permute-done.6.slab_ref, bf16[640,512]{1,0:T(8,128)(2,1)S(1)} %get-tuple-element.29.lanes_ref, bf16[16,128,256]{2,1,0:T(8,128)(2,1)S(1)} %get-tuple-element.30.band_ref, ...), custom_call_target="tpu_custom_call" | custom-call | flops 2147483648 | bytes 1048576 | tf_op jit(solution)/shard_map/pallas_call | solution.py:581
  (6 shorter events, 0.1 us)
Async XLA Ops:
  0.0 1.2 %copy-start = (bf16[64,64,128]{2,1,0:T(8,128)(2,1)S(1)}, bf16[64,64,128]{2,1,0:T(8,128)(2,1)}, u32[]{:S(2)}) copy-start(bf16[64,64,128]{2,1,0:T(8,128)(2,1)} %charges_ref.3) | copy-start | bytes 3145732
  1.2 22.7 %copy-start.1 = (bf16[64,64,128]{2,1,0:T(8,128)(2,1)S(1)}, bf16[64,64,128]{2,1,0:T(8,128)(2,1)}, u32[]{:S(2)}) copy-start(bf16[64,64,128]{2,1,0:T(8,128)(2,1)} %charges_ref.3) | copy-start | bytes 3145732
  1.2 12.1 %collective-permute-start.7 = (bf16[8,64,128]{2,1,0:T(8,128)(2,1)S(1)}, bf16[8,64,128]{2,1,0:T(8,128)(2,1)S(1)}, u32[]{:S(2)}, u32[]{:S(2)}) collective-permute-start(bf16[8,64,128]{2,1,0:T(8,128)(2,1)S(1)} %get-tuple-element.31), channel_id=1, source_target_pairs={{0,8},{8,16},{16,24},{24,0},{1,9},{9,17},{17,25},{25,1},{2,10},{10... | collective-permute-start | bytes 393224 | tf_op jit(solution)/shard_map/ppermute | solution.py:598
  4.4 9.0 %collective-permute-start.8 = (bf16[8,64,128]{2,1,0:T(8,128)(2,1)S(1)}, bf16[8,64,128]{2,1,0:T(8,128)(2,1)S(1)}, u32[]{:S(2)}, u32[]{:S(2)}) collective-permute-start(bf16[8,64,128]{2,1,0:T(8,128)(2,1)S(1)} %get-tuple-element.32), channel_id=1, source_target_pairs={{0,24},{8,0},{16,8},{24,16},{1,25},{9,1},{17,9},{25,17},{2,26},{10... | collective-permute-start | bytes 393224 | tf_op jit(solution)/shard_map/ppermute | solution.py:598
  9.4 10.9 %collective-permute-start = (bf16[624,128]{1,0:T(8,128)(2,1)S(1)}, bf16[624,128]{1,0:T(8,128)(2,1)S(1)}, u32[]{:S(2)}, u32[]{:S(2)}) collective-permute-start(bf16[624,128]{1,0:T(8,128)(2,1)S(1)} %get-tuple-element.20), channel_id=1, source_target_pairs={{0,8},{8,16},{16,24},{24,0},{1,9},{9,17},{17,25},{25,1},{2,10},{10... | collective-permute-start | bytes 479240 | tf_op jit(solution)/shard_map/ppermute | solution.py:598
  9.5 10.8 %collective-permute-start.1 = (bf16[624,128]{1,0:T(8,128)(2,1)S(1)}, bf16[624,128]{1,0:T(8,128)(2,1)S(1)}, u32[]{:S(2)}, u32[]{:S(2)}) collective-permute-start(bf16[624,128]{1,0:T(8,128)(2,1)S(1)} %get-tuple-element.21), channel_id=1, source_target_pairs={{0,24},{8,0},{16,8},{24,16},{1,25},{9,1},{17,9},{25,17},{2,26},{10... | collective-permute-start | bytes 479240 | tf_op jit(solution)/shard_map/ppermute | solution.py:598
  13.4 10.5 %collective-permute-start.10 = (bf16[80,8,128]{2,1,0:T(8,128)(2,1)S(1)}, bf16[80,8,128]{2,1,0:T(8,128)(2,1)S(1)}, u32[]{:S(2)}, u32[]{:S(2)}) collective-permute-start(bf16[80,8,128]{2,1,0:T(8,128)(2,1)S(1)} %pad_maximum_fusion.2), channel_id=1, source_target_pairs={{0,6},{2,0},{4,2},{6,4},{1,7},{3,1},{5,3},{7,5},{8,14},{10,8},{12,... | collective-permute-start | bytes 491528 | tf_op jit(solution)/shard_map/ppermute | solution.py:598
  13.6 10.4 %collective-permute-start.9 = (bf16[80,8,128]{2,1,0:T(8,128)(2,1)S(1)}, bf16[80,8,128]{2,1,0:T(8,128)(2,1)S(1)}, u32[]{:S(2)}, u32[]{:S(2)}) collective-permute-start(bf16[80,8,128]{2,1,0:T(8,128)(2,1)S(1)} %pad_maximum_fusion.1), channel_id=1, source_target_pairs={{0,2},{2,4},{4,6},{6,0},{1,3},{3,5},{5,7},{7,1},{8,10},{10,12},{12... | collective-permute-start | bytes 491528 | tf_op jit(solution)/shard_map/ppermute | solution.py:598
  14.1 6.3 %collective-permute-start.2 = (f32[3,16,128]{2,1,0:T(8,128)S(1)}, f32[3,16,128]{2,1,0:T(8,128)S(1)}, u32[]{:S(2)}, u32[]{:S(2)}) collective-permute-start(f32[3,16,128]{2,1,0:T(8,128)S(1)} %get-tuple-element.22), channel_id=1, source_target_pairs={{0,16},{8,24},{16,0},{24,8},{1,17},{9,25},{17,1},{25,9},{2,18},{10... | collective-permute-start | bytes 73736 | tf_op jit(solution)/shard_map/ppermute | solution.py:598
  20.3 9.8 %copy-start.2 = (bf16[1168,128]{1,0:T(8,128)(2,1)S(1)}, bf16[1168,128]{1,0:T(8,128)(2,1)}, u32[]{:S(2)}) copy-start(bf16[1168,128]{1,0:T(8,128)(2,1)} %constant.2.clone.refs_0_.table_ref) | copy-start | bytes 897028
  20.7 9.5 %collective-permute-start.3 = (bf16[1008,128]{1,0:T(8,128)(2,1)S(1)}, bf16[1008,128]{1,0:T(8,128)(2,1)S(1)}, u32[]{:S(2)}, u32[]{:S(2)}) collective-permute-start(bf16[1008,128]{1,0:T(8,128)(2,1)S(1)} %get-tuple-element.24), channel_id=1, source_target_pairs={{0,2},{2,4},{4,6},{6,0},{1,3},{3,5},{5,7},{7,1},{8,10},{10,12},{12... | collective-permute-start | bytes 774152 | tf_op jit(solution)/shard_map/ppermute | solution.py:598
  20.7 9.4 %collective-permute-start.4 = (bf16[1008,128]{1,0:T(8,128)(2,1)S(1)}, bf16[1008,128]{1,0:T(8,128)(2,1)S(1)}, u32[]{:S(2)}, u32[]{:S(2)}) collective-permute-start(bf16[1008,128]{1,0:T(8,128)(2,1)S(1)} %get-tuple-element.25), channel_id=1, source_target_pairs={{0,6},{2,0},{4,2},{6,4},{1,7},{3,1},{5,3},{7,5},{8,14},{10,8},{12,... | collective-permute-start | bytes 774152 | tf_op jit(solution)/shard_map/ppermute | solution.py:598
  22.5 10.2 %copy-start.3 = (f32[4,4,17]{2,1,0:T(4,128)S(1)}, f32[4,4,17]{2,1,0:T(4,128)}, u32[]{:S(2)}) copy-start(f32[4,4,17]{2,1,0:T(4,128)} %param.4) | copy-start | bytes 3268
  22.5 7.6 %collective-permute-start.5 = (f32[5,16,128]{2,1,0:T(8,128)S(1)}, f32[5,16,128]{2,1,0:T(8,128)S(1)}, u32[]{:S(2)}, u32[]{:S(2)}) collective-permute-start(f32[5,16,128]{2,1,0:T(8,128)S(1)} %get-tuple-element.26), channel_id=1, source_target_pairs={{0,4},{2,6},{4,0},{6,2},{1,5},{3,7},{5,1},{7,3},{8,12},{10,14},{12... | collective-permute-start | bytes 122888 | tf_op jit(solution)/shard_map/ppermute | solution.py:598
  24.7 11.9 %collective-permute-start.11 = (bf16[16,6400]{1,0:T(8,128)(2,1)S(1)}, bf16[16,6400]{1,0:T(8,128)(2,1)S(1)}, u32[]{:S(2)}, u32[]{:S(2)}) collective-permute-start(bf16[16,6400]{1,0:T(8,128)(2,1)S(1)} %shard_map.42), channel_id=1, source_target_pairs={{0,1},{1,0},{2,3},{3,2},{4,5},{5,4},{6,7},{7,6},{8,9},{9,8},{10,11... | collective-permute-start | bytes 614408 | tf_op jit(solution)/shard_map/ppermute | solution.py:598
  31.1 14.6 %collective-permute-start.6 = (bf16[32,8960]{1,0:T(8,128)(2,1)S(1)}, bf16[32,8960]{1,0:T(8,128)(2,1)S(1)}, u32[]{:S(2)}, u32[]{:S(2)}) collective-permute-start(bf16[32,8960]{1,0:T(8,128)(2,1)S(1)} %get-tuple-element.28), channel_id=1, source_target_pairs={{0,1},{1,0},{2,3},{3,2},{4,5},{5,4},{6,7},{7,6},{8,9},{9,8},{10,11... | collective-permute-start | bytes 1720328 | tf_op jit(solution)/shard_map/ppermute | solution.py:598

commit v2 on v1

--- a/solution.py
+++ b/solution.py
@@ -39,11 +39,11 @@
 
 def levels_of(block):
     levels = [Level(index, block) for index in range(4)]
-    lane, start = 0, 0
+    lane = 0
     for level in levels[1:]:
-        level.lane, level.start = lane, start
+        level.lane = lane
         lane += level.win[2]
-        start += level.span
+    levels[3].start = levels[2].span
     assert lane <= LANES and block[2] == LANES
     assert all(level.n[d] % 8 == 0 for level in levels for d in range(3))
     return levels
@@ -366,8 +366,8 @@
 
 
 def lanes_kernel(levels, table, x_ref, prev_ref, next_ref, far_prev_ref, *refs):
-    far_next_ref = far_prev_ref if len(refs) == 3 else refs[0]
-    table_ref, flat_ref, slab_ref = refs[-3:]
+    far_next_ref = far_prev_ref if len(refs) == 5 else refs[0]
+    table_ref, flat_refs, slab_refs = refs[-5], refs[-4:-2], refs[-2:]
 
     def block_of(ref, block):
         return ref[block * SLAB : (block + 1) * SLAB].astype(F32)
@@ -381,6 +381,7 @@
 
     for level, mask in zip(levels[1:], lane_masks(levels)):
         blocks, step = level.inp[1] // 8, level.n[1] // 8
+        flat_ref = flat_refs[level.index > 1]
         for at in range(level.full[0]):
             own = x_ref[plane_at(levels, level, at, "full")]
             slabs = [received(prev_ref, at, level), received(next_ref, at, level)]
@@ -403,8 +404,9 @@
         last = level.start + level.span
         if used < last:
             flat_ref[used:last] = jnp.zeros((last - used, LANES), F32)
-    shift = levels[-1].start + levels[-1].span - levels[2].start
+    shift = levels[2].span + levels[3].span
     for level in levels[1:]:
+        flat_ref, slab_ref = flat_refs[level.index > 1], slab_refs[level.index > 1]
         send = table.get(table_ref, "send", level.index)
         for first in range(level.start, level.start + level.span, 512):
             stop = min(first + 512, level.start + level.span)
@@ -437,7 +439,7 @@
             for term in range(4):
                 halves = [
                     first_ref[
-                        pl.ds(pair * 16 + 8 * half, 8),
+                        slice(pair * 16 + 8 * half, pair * 16 + 8 * half + 8),
                         TILE * block : TILE * block + 32,
                         term_lanes(term),
                     ].reshape(256, LANES)
@@ -445,7 +447,7 @@
                 ]
                 result = dot(band(term), jnp.concatenate(halves, 1))
                 second_ref[
-                    term, TILE * block : TILE * (block + 1), pl.ds(pl.multiple_of(pair * 16, 16), 16)
+                    term, TILE * block : TILE * (block + 1), slice(pair * 16, pair * 16 + 16)
                 ] = parts_of(result).astype(BF16)
 
     def along_x(pair):
@@ -454,7 +456,7 @@
             for term in range(4):
                 halves = [
                     second_ref[
-                        term, pl.ds(pair * 16 + 8 * half, 8), TILE * block : TILE * block + 32
+                        term, slice(pair * 16 + 8 * half, pair * 16 + 8 * half + 8), TILE * block : TILE * block + 32
                     ].reshape(256, LANES)
                     for half in range(2)
                 ]
@@ -462,12 +464,14 @@
                 result = part if result is None else result + part
             put(block, pair, parts_of(result))
 
-    pl.loop(0, level.inp[0] // 16)(along_y)
-    pl.loop(0, level.out[1] // 16)(along_x)
+    for pair in range(level.inp[0] // 16):
+        along_y(pair)
+    for pair in range(level.out[1] // 16):
+        along_x(pair)
 
 
 def fine_kernel(level, wide_ref, halo_ref, lanes_ref, band_ref, out_ref, first_ref, second_ref):
-    rows, step = level.inp[1], 8
+    rows, step = level.inp[1], 16
     row = lax.broadcasted_iota(jnp.int32, (2 * REACH, LANES), 0)
     lane = lax.broadcasted_iota(jnp.int32, (2 * REACH, LANES), 1)
     place = jnp.where(lane == row, 1.0, 0.0).astype(BF16)
@@ -481,40 +485,50 @@
         first_ref[pl.ds(chunk * step, step)] = result.astype(BF16).reshape(step, rows, 4 * LANES)
 
     def put(block, pair, value):
-        out_ref[TILE * block : TILE * (block + 1), pl.ds(pl.multiple_of(pair * 16, 16), 16)] = value
+        out_ref[TILE * block : TILE * (block + 1), slice(pair * 16, pair * 16 + 16)] = value
 
     two_passes(level, lambda term: band_ref[term], first_ref, second_ref, put)
 
 
-def coarse_kernel(levels, table, flat_ref, slab_ref, lanes_ref, band_ref, table_ref, fine_ref, *refs):
-    out_ref, first_refs, second_refs, sum_refs = refs[0], refs[1:4], refs[4:7], refs[7:10]
-    shift = levels[-1].start + levels[-1].span - levels[2].start
-    for level in reversed(levels[1:]):
-        which = level.index - 1
-        first_ref, sum_ref = first_refs[which], sum_refs[which]
-        rows, step = level.inp[1], 4
-        first_lane, _ = lane_rows(level)
-        place = table.get(table_ref, "place", level.index)
-        for plane in range(0, level.full[0], step):
-            count = min(step, level.full[0] - plane)
-            if (count * rows) % LANES:
-                count += 1
-            start, stop = level.start + plane * rows, level.start + (plane + count) * rows
-            slab = slab_ref[:, start:stop]
-            if level.index > 1:
-                slab = jnp.concatenate([slab, slab_ref[:, start + shift : stop + shift]], 0)
-            value = flat_ref[start:stop] + dot(slab, place, ((0,), (0,)))
-            result = dot(value.astype(BF16), lanes_ref[first_lane : first_lane + LANES])
-            first_ref[plane : plane + count] = result.astype(BF16).reshape(count, rows, 4 * LANES)
-        rest = level.inp[0] - plane - count
-        if rest > 0:
-            first_ref[plane + count :] = jnp.zeros((rest, rows, 4 * LANES), BF16)
-
-        def put(block, pair, value, sum_ref=sum_ref):
-            sum_ref[TILE * block : TILE * (block + 1), pl.ds(pl.multiple_of(pair * 16, 16), 16)] = value
-
-        base = 4 * level.index
-        two_passes(level, lambda term, base=base: band_ref[base + term], first_ref, second_refs[which], put)
+def level_passes(levels, level, table, flat_ref, slab_ref, lanes_ref, band_ref, table_ref, first_ref, second_ref, sum_ref):
+    shift = levels[2].span + levels[3].span
+    rows, step = level.inp[1], 4
+    first_lane, _ = lane_rows(level)
+    place = table.get(table_ref, "place", level.index)
+    for plane in range(0, level.full[0], step):
+        count = min(step, level.full[0] - plane)
+        if (count * rows) % LANES:
+            count += 1
+        start, stop = level.start + plane * rows, level.start + (plane + count) * rows
+        slab = slab_ref[:, start:stop]
+        if level.index > 1:
+            slab = jnp.concatenate([slab, slab_ref[:, start + shift : stop + shift]], 0)
+        value = flat_ref[start:stop] + dot(slab, place, ((0,), (0,)))
+        result = dot(value.astype(BF16), lanes_ref[first_lane : first_lane + LANES])
+        first_ref[plane : plane + count] = result.astype(BF16).reshape(count, rows, 4 * LANES)
+    rest = level.inp[0] - plane - count
+    if rest > 0:
+        first_ref[plane + count :] = jnp.zeros((rest, rows, 4 * LANES), BF16)
+
+    def put(block, pair, value):
+        sum_ref[TILE * block : TILE * (block + 1), slice(pair * 16, pair * 16 + 16)] = value
+
+    base = 4 * level.index
+    two_passes(level, lambda term: band_ref[base + term], first_ref, second_ref, put)
+
+
+def middle_kernel(levels, table, flat_ref, slab_ref, lanes_ref, band_ref, table_ref, sum_ref, first_ref, second_ref):
+    level_passes(levels, levels[1], table, flat_ref, slab_ref, lanes_ref, band_ref, table_ref, first_ref, second_ref, sum_ref)
+
+
+def coarse_kernel(levels, table, flat_ref, slab_ref, lanes_ref, band_ref, table_ref, middle_ref, fine_ref, *refs):
+    out_ref, first_refs, second_refs, sum_refs = refs[0], refs[1:3], refs[3:5], refs[5:8]
+    for level in (levels[3], levels[2]):
+        which = level.index - 2
+        level_passes(
+            levels, level, table, flat_ref, slab_ref, lanes_ref, band_ref, table_ref,
+            first_refs[which], second_refs[which], sum_refs[level.index - 1],
+        )
 
     def stretch(fine, coarse, source):
         planes, rows, _ = source.shape
@@ -543,7 +557,7 @@
         def emit(at, value, fine=fine, sum_ref=sum_ref):
             plane = at + fine.low
             if 0 <= plane < fine.win[0]:
-                sum_ref[plane] = sum_ref[plane] + value
+                sum_ref[plane] = (middle_ref if fine.index == 1 else sum_ref)[plane] + value
 
         for half in range(-1, (fine.n[0] + fine.high + 1) // 2):
             prolong(fine, coarse, [half], source, emit)
@@ -674,17 +688,16 @@
     )
     halo = z_pair(sides, "gz")
 
-    flat_rows = sum(level.span for level in coarse)
-    flat, slabs = call(
+    spans = (coarse[0].span, coarse[1].span + coarse[2].span)
+    *flats, slab_one, slab_two = call(
         functools.partial(lanes_kernel, levels, table),
-        [
-            shape((flat_rows, LANES), F32),
-            shape((2 * SLAB, 2 * flat_rows - levels[1].span), BF16),
-        ],
+        [shape((span, LANES), F32) for span in spans]
+        + [shape((2 * SLAB, count), BF16) for count in (spans[0], 2 * spans[1])],
         [r, m_prev, m_next, *far, table_array],
         flops=1 << 26,
     )
-    slabs = z_pair(slabs, "gz")
+    slab_one = z_pair(slab_one, "gz")
+    slab_two = z_pair(slab_two, "gz")
 
     fine = call(
         functools.partial(fine_kernel, zero),
@@ -695,17 +708,30 @@
             pltpu.VMEM((4, zero.out[1], zero.inp[0], LANES), BF16),
         ],
         flops=1 << 32,
-        limit=24,
+        limit=20,
+    )
+    slab_one, fine = lax.optimization_barrier((slab_one, fine))
+
+    def scratch(some):
+        return [pltpu.VMEM((*lv.inp, 4 * LANES), BF16) for lv in some] + [
+            pltpu.VMEM((4, lv.out[1], lv.inp[0], LANES), BF16) for lv in some
+        ]
+
+    middle = call(
+        functools.partial(middle_kernel, levels, table),
+        shape((*coarse[0].out, LANES), F32),
+        [flats[0], slab_one, lanes, band, table_array],
+        scratch=scratch(coarse[:1]),
+        flops=1 << 31,
+        limit=16,
     )
     return call(
         functools.partial(coarse_kernel, levels, table),
         shape(charges.shape, BF16),
-        [flat, slabs, lanes, band, table_array, fine],
-        scratch=[pltpu.VMEM((*lv.inp, 4 * LANES), BF16) for lv in coarse]
-        + [pltpu.VMEM((4, lv.out[1], lv.inp[0], LANES), BF16) for lv in coarse]
-        + [pltpu.VMEM((*lv.out, LANES), F32) for lv in coarse],
-        flops=1 << 31,
-        limit=30,
+        [flats[1], slab_two, lanes, band, table_array, middle, fine],
+        scratch=scratch(coarse[1:]) + [pltpu.VMEM((*lv.out, LANES), F32) for lv in coarse],
+        flops=1 << 30,
+        limit=16,
     )
 
 

time: 60.5 us -> 61.2 us (1.012)
  waiting for transfers between devices: 10.3 us -> 15.9 us
  Pallas kernels: 32.4 us -> 27 us
    ppermute x12 -> x13, waiting for transfers between devices: 10.3 us -> 15.9 us  [shifted(): lax.ppermute(value, axis, [(i, (i + by) % count) for i in range(count)])]
    pallas_call x8 -> x9, Pallas kernels: 32.4 us -> 27 us  [call(): pl.pallas_call(kernel, out_shape=out_shape, in_specs=specs, out_specs=out...]
    ppermute x12 -> x13, starting transfers between devices: 16.1 us -> 16.5 us  [shifted(): lax.ppermute(value, axis, [(i, (i + by) % count) for i in range(count)])]
  transfers between devices with their start and end apart: 12 -> 13, of which waited for: 3 -> 5; matrix products, arithmetic and copies ran while one was open for 0% -> 0% of each run, Pallas kernels for 29% -> 32%
where the time goes in v2:
time: 61.2 us; the launch traced here: 61 us
  Pallas kernels  27 us (44%)
  starting transfers between devices  16.5 us (27%)
  waiting for transfers between devices  15.9 us (26%)
  local copies, waits for them, and re-layouts  1.29 us (2%)
    pallas_call x9, Pallas kernels, call(): pl.pallas_call(kernel, out_shape=out_shape, in_specs=specs, out_specs=out...  27 us
    ppermute x13, starting transfers between devices, shifted(): lax.ppermute(value, axis, [(i, (i + by) % count) for i in range(count)])  16.5 us
    ppermute x13, waiting for transfers between devices, shifted(): lax.ppermute(value, axis, [(i, (i + by) % count) for i in range(count)])  15.9 us
    unnamed x8, local copies, waits for them, and re-layouts  1.24 us
  transfers between devices with their start and end apart: 13, of which 5 were waited for; matrix products, arithmetic and copies ran while one was open for 0% of the time, Pallas kernels for 32%

profile of v2, /device:TPU:0, one launch (start us, length us, event | category | flops | bytes accessed | tf_op | source)
XLA Modules:
  0.0 61.0 jit_solution(3999558101448511024)
XLA Ops:
  0.0 0.0 copy-start
  0.0 1.2 %copy-done = bf16[64,64,128]{2,1,0:T(8,128)(2,1)S(1)} copy-done((bf16[64,64,128]{2,1,0:T(8,128)(2,1)S(1)}, bf16[64,64,128]{2,1,0:T(8,128)(2,1)}, u32[]{:S(2)}) %copy-start) | copy-done | bytes 1048600
  1.2 3.1 %collective-permute-start.8 = (bf16[8,64,128]{2,1,0:T(8,128)(2,1)S(1)}, bf16[8,64,128]{2,1,0:T(8,128)(2,1)S(1)}, u32[]{:S(2)}, u32[]{:S(2)}) collective-permute-start(bf16[8,64,128]{2,1,0:T(8,128)(2,1)S(1)} %get-tuple-element.37), channel_id=1, source_target_pairs={{0,8},{8,16},{16,24},{24,0},{1,9},{9,17},{17,25},{25,1},{2,10},{10... | collective-permute-start | bytes 393224 | tf_op jit(solution)/shard_map/ppermute | solution.py:612
  4.4 2.1 %collective-permute-start.9 = (bf16[8,64,128]{2,1,0:T(8,128)(2,1)S(1)}, bf16[8,64,128]{2,1,0:T(8,128)(2,1)S(1)}, u32[]{:S(2)}, u32[]{:S(2)}) collective-permute-start(bf16[8,64,128]{2,1,0:T(8,128)(2,1)S(1)} %get-tuple-element.38), channel_id=1, source_target_pairs={{0,24},{8,0},{16,8},{24,16},{1,25},{9,1},{17,9},{25,17},{2,26},{10... | collective-permute-start | bytes 393224 | tf_op jit(solution)/shard_map/ppermute | solution.py:612
  6.5 0.0 copy-start.1
  6.5 4.2 %collective-permute-done.8 = bf16[8,64,128]{2,1,0:T(8,128)(2,1)S(1)} collective-permute-done((bf16[8,64,128]{2,1,0:T(8,128)(2,1)S(1)}, bf16[8,64,128]{2,1,0:T(8,128)(2,1)S(1)}, u32[]{:S(2)}, u32[]{:S(2)}) %collective-permute-start.8) | collective-permute-done | bytes 131104 | tf_op jit(solution)/shard_map/ppermute | solution.py:612
  10.7 1.4 %collective-permute-done.9 = bf16[8,64,128]{2,1,0:T(8,128)(2,1)S(1)} collective-permute-done((bf16[8,64,128]{2,1,0:T(8,128)(2,1)S(1)}, bf16[8,64,128]{2,1,0:T(8,128)(2,1)S(1)}, u32[]{:S(2)}, u32[]{:S(2)}) %collective-permute-start.9) | collective-permute-done | bytes 131104 | tf_op jit(solution)/shard_map/ppermute | solution.py:612
  12.2 0.6 collective-permute-start.11
  12.8 0.1 collective-permute-start.10
  12.8 3.0 %shard_map.37 = (f32[2112,128]{1,0:T(8,128)S(1)}, bf16[624,128]{1,0:T(8,128)(2,1)S(1)}, bf16[624,128]{1,0:T(8,128)(2,1)S(1)}, f32[3,16,128]{2,1,0:T(8,128)S(1)}) custom-call(bf16[64,64,128]{2,1,0:T(8,128)(2,1)S(1)} %copy-done), custom_call_target="tpu_custom_call" | custom-call | flops 134217728 | bytes 1048576 | tf_op jit(solution)/shard_map/pallas_call | solution.py:595
  15.8 1.7 %collective-permute-start = (bf16[624,128]{1,0:T(8,128)(2,1)S(1)}, bf16[624,128]{1,0:T(8,128)(2,1)S(1)}, u32[]{:S(2)}, u32[]{:S(2)}) collective-permute-start(bf16[624,128]{1,0:T(8,128)(2,1)S(1)} %get-tuple-element.24), channel_id=1, source_target_pairs={{0,8},{8,16},{16,24},{24,0},{1,9},{9,17},{17,25},{25,1},{2,10},{10... | collective-permute-start | bytes 479240 | tf_op jit(solution)/shard_map/ppermute | solution.py:612
  17.5 2.1 %collective-permute-start.1 = (bf16[624,128]{1,0:T(8,128)(2,1)S(1)}, bf16[624,128]{1,0:T(8,128)(2,1)S(1)}, u32[]{:S(2)}, u32[]{:S(2)}) collective-permute-start(bf16[624,128]{1,0:T(8,128)(2,1)S(1)} %get-tuple-element.25), channel_id=1, source_target_pairs={{0,24},{8,0},{16,8},{24,16},{1,25},{9,1},{17,9},{25,17},{2,26},{10... | collective-permute-start | bytes 479240 | tf_op jit(solution)/shard_map/ppermute | solution.py:612
  19.7 0.0 collective-permute-start.2
  19.7 8.2 %collective-permute-done.2.far_prev_ref = f32[3,16,128]{2,1,0:T(8,128)S(1)} collective-permute-done((f32[3,16,128]{2,1,0:T(8,128)S(1)}, f32[3,16,128]{2,1,0:T(8,128)S(1)}, u32[]{:S(2)}, u32[]{:S(2)}) %collective-permute-start.2) | collective-permute-done | bytes 24608 | tf_op jit(solution)/shard_map/ppermute | solution.py:612
  27.9 0.0 collective-permute-done.prev_ref
  27.9 0.0 collective-permute-done.1.next_ref
  27.9 0.3 shard_map.38
  28.3 0.1 collective-permute-start.3
  28.3 1.7 %collective-permute-start.4 = (bf16[1008,128]{1,0:T(8,128)(2,1)S(1)}, bf16[1008,128]{1,0:T(8,128)(2,1)S(1)}, u32[]{:S(2)}, u32[]{:S(2)}) collective-permute-start(bf16[1008,128]{1,0:T(8,128)(2,1)S(1)} %get-tuple-element.29), channel_id=1, source_target_pairs={{0,6},{2,0},{4,2},{6,4},{1,7},{3,1},{5,3},{7,5},{8,14},{10,8},{12,... | collective-permute-start | bytes 774152 | tf_op jit(solution)/shard_map/ppermute | solution.py:612
  30.1 0.0 collective-permute-done.11
  30.1 0.0 collective-permute-done.10
  30.1 0.0 copy-done.1
  30.1 0.2 pad_maximum_fusion.wide_ref
  30.3 0.0 copy-start.3
  30.3 0.0 copy-start.2
  30.3 0.6 shard_map.42
  30.9 1.6 %collective-permute-start.12 = (bf16[16,6400]{1,0:T(8,128)(2,1)S(1)}, bf16[16,6400]{1,0:T(8,128)(2,1)S(1)}, u32[]{:S(2)}, u32[]{:S(2)}) collective-permute-start(bf16[16,6400]{1,0:T(8,128)(2,1)S(1)} %shard_map.42), channel_id=1, source_target_pairs={{0,1},{1,0},{2,3},{3,2},{4,5},{5,4},{6,7},{7,6},{8,9},{9,8},{10,11... | collective-permute-start | bytes 614408 | tf_op jit(solution)/shard_map/ppermute | solution.py:612
  32.4 1.4 %collective-permute-start.5 = (f32[5,16,128]{2,1,0:T(8,128)S(1)}, f32[5,16,128]{2,1,0:T(8,128)S(1)}, u32[]{:S(2)}, u32[]{:S(2)}) collective-permute-start(f32[5,16,128]{2,1,0:T(8,128)S(1)} %get-tuple-element.30), channel_id=1, source_target_pairs={{0,4},{2,6},{4,0},{6,2},{1,5},{3,7},{5,1},{7,3},{8,12},{10,14},{12... | collective-permute-start | bytes 122888 | tf_op jit(solution)/shard_map/ppermute | solution.py:612
  33.9 0.0 copy-done.3
  33.9 4.1 %shard_map.40 = (bf16[16,128,256]{2,1,0:T(8,128)(2,1)S(1)}, bf16[640,512]{1,0:T(8,128)(2,1)S(1)}) custom-call(f32[16,17]{1,0:T(8,128)S(1)} %bitcast.1), custom_call_target="tpu_custom_call" | custom-call | flops 67108864 | bytes 1048576 | tf_op jit(solution)/shard_map/pallas_call | solution.py:595
  38.0 0.0 collective-permute-done.5.far_prev_ref
  38.0 0.0 collective-permute-done.3.prev_ref
  38.0 0.0 collective-permute-done.4.next_ref
  38.0 0.0 copy-done.2
  38.0 1.0 %shard_map.39 = (f32[3328,128]{1,0:T(8,128)S(1)}, f32[2816,128]{1,0:T(8,128)S(1)}, bf16[32,3328]{1,0:T(8,128)(2,1)S(1)}, bf16[32,5632]{1,0:T(8,128)(2,1)S(1)}) custom-call(f32[3392,128]{1,0:T(8,128)S(1)} %get-tuple-element.27.x_ref, bf16[1008,128]{1,0:T(8,128)(2,1)S(1)} %collective-permute-done.3.prev_ref, ...), custom_call_target="tpu_custom_call" | custom-call | flops 67108864 | bytes 1048576 | tf_op jit(solution)/shard_map/pallas_call | solution.py:595
  39.0 1.3 %collective-permute-start.7 = (bf16[32,3328]{1,0:T(8,128)(2,1)S(1)}, bf16[32,3328]{1,0:T(8,128)(2,1)S(1)}, u32[]{:S(2)}, u32[]{:S(2)}) collective-permute-start(bf16[32,3328]{1,0:T(8,128)(2,1)S(1)} %get-tuple-element.36), channel_id=1, source_target_pairs={{0,1},{1,0},{2,3},{3,2},{4,5},{5,4},{6,7},{7,6},{8,9},{9,8},{10,11... | collective-permute-start | bytes 638984 | tf_op jit(solution)/shard_map/ppermute | solution.py:612
  40.3 0.8 %collective-permute-start.6 = (bf16[32,5632]{1,0:T(8,128)(2,1)S(1)}, bf16[32,5632]{1,0:T(8,128)(2,1)S(1)}, u32[]{:S(2)}, u32[]{:S(2)}) collective-permute-start(bf16[32,5632]{1,0:T(8,128)(2,1)S(1)} %get-tuple-element.32), channel_id=1, source_target_pairs={{0,1},{1,0},{2,3},{3,2},{4,5},{5,4},{6,7},{7,6},{8,9},{9,8},{10,11... | collective-permute-start | bytes 1081352 | tf_op jit(solution)/shard_map/ppermute | solution.py:612
  41.1 0.0 collective-permute-done.12.halo_ref
  41.1 5.9 %shard_map.43.fine_ref = f32[64,64,128]{2,1,0:T(8,128)S(1)} custom-call(bf16[80,80,128]{2,1,0:T(8,128)(2,1)S(1)} %pad_maximum_fusion.wide_ref, bf16[16,6400]{1,0:T(8,128)(2,1)S(1)} %collective-permute-done.12.halo_ref, bf16[640,512]{1,0:T(8,128)(2,1)S(1)} %get-tuple-element.33.lanes_ref, bf16[16,128,256]{2,1,0:T(8,128)(2,1)S(1)} %get-tuple-element.34.band_ref), custom_call_target="tpu_custom_call" | custom-call | flops 4294967296 | bytes 1048576 | tf_op jit(solution)/shard_map/pallas_call | solution.py:595
  47.1 0.1 collective-permute-done.7.slab_ref
  47.2 4.3 %shard_map.44.middle_ref = f32[48,48,128]{2,1,0:T(8,128)S(1)} custom-call(f32[3328,128]{1,0:T(8,128)S(1)} %get-tuple-element.35.flat_ref, bf16[32,3328]{1,0:T(8,128)(2,1)S(1)} %collective-permute-done.7.slab_ref, bf16[640,512]{1,0:T(8,128)(2,1)S(1)} %get-tuple-element.33.lanes_ref, bf16[16,128,256]{2,1,0:T(8,128)(2,1)S(1)} %get-tuple-element.34.band_ref, ...), custom_call_target="tpu_custom_call" | custom-call | flops 2147483648 | bytes 1048576 | tf_op jit(solution)/shard_map/pallas_call | solution.py:595
  51.5 1.9 %collective-permute-done.6.slab_ref = bf16[32,5632]{1,0:T(8,128)(2,1)S(1)} collective-permute-done((bf16[32,5632]{1,0:T(8,128)(2,1)S(1)}, bf16[32,5632]{1,0:T(8,128)(2,1)S(1)}, u32[]{:S(2)}, u32[]{:S(2)}) %collective-permute-start.6) | collective-permute-done | bytes 360480 | tf_op jit(solution)/shard_map/ppermute | solution.py:612
  53.3 7.7 %shard_map.45 = bf16[64,64,128]{2,1,0:T(8,128)(2,1)} custom-call(f32[2816,128]{1,0:T(8,128)S(1)} %get-tuple-element.31.flat_ref, bf16[32,5632]{1,0:T(8,128)(2,1)S(1)} %collective-permute-done.6.slab_ref, bf16[640,512]{1,0:T(8,128)(2,1)S(1)} %get-tuple-element.33.lanes_ref, bf16[16,128,256]{2,1,0:T(8,128)(2,1)S(1)} %get-tuple-element.34.band_ref, ...), custom_call_target="tpu_custom_call" | custom-call | flops 1073741824 | bytes 1048576 | tf_op jit(solution)/shard_map/pallas_call | solution.py:595
  (6 shorter events, 0.1 us)
Async XLA Ops:
  0.0 1.2 %copy-start = (bf16[64,64,128]{2,1,0:T(8,128)(2,1)S(1)}, bf16[64,64,128]{2,1,0:T(8,128)(2,1)}, u32[]{:S(2)}) copy-start(bf16[64,64,128]{2,1,0:T(8,128)(2,1)} %charges_ref.3) | copy-start | bytes 3145732
  1.2 9.5 %collective-permute-start.8 = (bf16[8,64,128]{2,1,0:T(8,128)(2,1)S(1)}, bf16[8,64,128]{2,1,0:T(8,128)(2,1)S(1)}, u32[]{:S(2)}, u32[]{:S(2)}) collective-permute-start(bf16[8,64,128]{2,1,0:T(8,128)(2,1)S(1)} %get-tuple-element.37), channel_id=1, source_target_pairs={{0,8},{8,16},{16,24},{24,0},{1,9},{9,17},{17,25},{25,1},{2,10},{10... | collective-permute-start | bytes 393224 | tf_op jit(solution)/shard_map/ppermute | solution.py:612
  4.4 7.8 %collective-permute-start.9 = (bf16[8,64,128]{2,1,0:T(8,128)(2,1)S(1)}, bf16[8,64,128]{2,1,0:T(8,128)(2,1)S(1)}, u32[]{:S(2)}, u32[]{:S(2)}) collective-permute-start(bf16[8,64,128]{2,1,0:T(8,128)(2,1)S(1)} %get-tuple-element.38), channel_id=1, source_target_pairs={{0,24},{8,0},{16,8},{24,16},{1,25},{9,1},{17,9},{25,17},{2,26},{10... | collective-permute-start | bytes 393224 | tf_op jit(solution)/shard_map/ppermute | solution.py:612
  6.5 23.6 %copy-start.1 = (bf16[64,64,128]{2,1,0:T(8,128)(2,1)S(1)}, bf16[64,64,128]{2,1,0:T(8,128)(2,1)}, u32[]{:S(2)}) copy-start(bf16[64,64,128]{2,1,0:T(8,128)(2,1)} %charges_ref.3) | copy-start | bytes 3145732
  12.2 17.9 %collective-permute-start.11 = (bf16[80,8,128]{2,1,0:T(8,128)(2,1)S(1)}, bf16[80,8,128]{2,1,0:T(8,128)(2,1)S(1)}, u32[]{:S(2)}, u32[]{:S(2)}) collective-permute-start(bf16[80,8,128]{2,1,0:T(8,128)(2,1)S(1)} %pad_maximum_fusion.2), channel_id=1, source_target_pairs={{0,6},{2,0},{4,2},{6,4},{1,7},{3,1},{5,3},{7,5},{8,14},{10,8},{12,... | collective-permute-start | bytes 491528 | tf_op jit(solution)/shard_map/ppermute | solution.py:612
  12.8 17.3 %collective-permute-start.10 = (bf16[80,8,128]{2,1,0:T(8,128)(2,1)S(1)}, bf16[80,8,128]{2,1,0:T(8,128)(2,1)S(1)}, u32[]{:S(2)}, u32[]{:S(2)}) collective-permute-start(bf16[80,8,128]{2,1,0:T(8,128)(2,1)S(1)} %pad_maximum_fusion.1), channel_id=1, source_target_pairs={{0,2},{2,4},{4,6},{6,0},{1,3},{3,5},{5,7},{7,1},{8,10},{10,12},{12... | collective-permute-start | bytes 491528 | tf_op jit(solution)/shard_map/ppermute | solution.py:612
  15.8 12.1 %collective-permute-start = (bf16[624,128]{1,0:T(8,128)(2,1)S(1)}, bf16[624,128]{1,0:T(8,128)(2,1)S(1)}, u32[]{:S(2)}, u32[]{:S(2)}) collective-permute-start(bf16[624,128]{1,0:T(8,128)(2,1)S(1)} %get-tuple-element.24), channel_id=1, source_target_pairs={{0,8},{8,16},{16,24},{24,0},{1,9},{9,17},{17,25},{25,1},{2,10},{10... | collective-permute-start | bytes 479240 | tf_op jit(solution)/shard_map/ppermute | solution.py:612
  17.5 10.4 %collective-permute-start.1 = (bf16[624,128]{1,0:T(8,128)(2,1)S(1)}, bf16[624,128]{1,0:T(8,128)(2,1)S(1)}, u32[]{:S(2)}, u32[]{:S(2)}) collective-permute-start(bf16[624,128]{1,0:T(8,128)(2,1)S(1)} %get-tuple-element.25), channel_id=1, source_target_pairs={{0,24},{8,0},{16,8},{24,16},{1,25},{9,1},{17,9},{25,17},{2,26},{10... | collective-permute-start | bytes 479240 | tf_op jit(solution)/shard_map/ppermute | solution.py:612
  19.7 8.2 %collective-permute-start.2 = (f32[3,16,128]{2,1,0:T(8,128)S(1)}, f32[3,16,128]{2,1,0:T(8,128)S(1)}, u32[]{:S(2)}, u32[]{:S(2)}) collective-permute-start(f32[3,16,128]{2,1,0:T(8,128)S(1)} %get-tuple-element.26), channel_id=1, source_target_pairs={{0,16},{8,24},{16,0},{24,8},{1,17},{9,25},{17,1},{25,9},{2,18},{10... | collective-permute-start | bytes 73736 | tf_op jit(solution)/shard_map/ppermute | solution.py:612
  28.3 9.7 %collective-permute-start.3 = (bf16[1008,128]{1,0:T(8,128)(2,1)S(1)}, bf16[1008,128]{1,0:T(8,128)(2,1)S(1)}, u32[]{:S(2)}, u32[]{:S(2)}) collective-permute-start(bf16[1008,128]{1,0:T(8,128)(2,1)S(1)} %get-tuple-element.28), channel_id=1, source_target_pairs={{0,2},{2,4},{4,6},{6,0},{1,3},{3,5},{5,7},{7,1},{8,10},{10,12},{12... | collective-permute-start | bytes 774152 | tf_op jit(solution)/shard_map/ppermute | solution.py:612
  28.3 9.7 %collective-permute-start.4 = (bf16[1008,128]{1,0:T(8,128)(2,1)S(1)}, bf16[1008,128]{1,0:T(8,128)(2,1)S(1)}, u32[]{:S(2)}, u32[]{:S(2)}) collective-permute-start(bf16[1008,128]{1,0:T(8,128)(2,1)S(1)} %get-tuple-element.29), channel_id=1, source_target_pairs={{0,6},{2,0},{4,2},{6,4},{1,7},{3,1},{5,3},{7,5},{8,14},{10,8},{12,... | collective-permute-start | bytes 774152 | tf_op jit(solution)/shard_map/ppermute | solution.py:612
  30.3 3.6 %copy-start.3 = (f32[4,4,17]{2,1,0:T(4,128)S(1)}, f32[4,4,17]{2,1,0:T(4,128)}, u32[]{:S(2)}) copy-start(f32[4,4,17]{2,1,0:T(4,128)} %param.4) | copy-start | bytes 3268
  30.3 7.7 %copy-start.2 = (bf16[1168,128]{1,0:T(8,128)(2,1)S(1)}, bf16[1168,128]{1,0:T(8,128)(2,1)}, u32[]{:S(2)}) copy-start(bf16[1168,128]{1,0:T(8,128)(2,1)} %constant.2.clone.refs_0_.table_ref) | copy-start | bytes 897028
  30.9 10.2 %collective-permute-start.12 = (bf16[16,6400]{1,0:T(8,128)(2,1)S(1)}, bf16[16,6400]{1,0:T(8,128)(2,1)S(1)}, u32[]{:S(2)}, u32[]{:S(2)}) collective-permute-start(bf16[16,6400]{1,0:T(8,128)(2,1)S(1)} %shard_map.42), channel_id=1, source_target_pairs={{0,1},{1,0},{2,3},{3,2},{4,5},{5,4},{6,7},{7,6},{8,9},{9,8},{10,11... | collective-permute-start | bytes 614408 | tf_op jit(solution)/shard_map/ppermute | solution.py:612
  32.4 5.5 %collective-permute-start.5 = (f32[5,16,128]{2,1,0:T(8,128)S(1)}, f32[5,16,128]{2,1,0:T(8,128)S(1)}, u32[]{:S(2)}, u32[]{:S(2)}) collective-permute-start(f32[5,16,128]{2,1,0:T(8,128)S(1)} %get-tuple-element.30), channel_id=1, source_target_pairs={{0,4},{2,6},{4,0},{6,2},{1,5},{3,7},{5,1},{7,3},{8,12},{10,14},{12... | collective-permute-start | bytes 122888 | tf_op jit(solution)/shard_map/ppermute | solution.py:612
  39.0 8.2 %collective-permute-start.7 = (bf16[32,3328]{1,0:T(8,128)(2,1)S(1)}, bf16[32,3328]{1,0:T(8,128)(2,1)S(1)}, u32[]{:S(2)}, u32[]{:S(2)}) collective-permute-start(bf16[32,3328]{1,0:T(8,128)(2,1)S(1)} %get-tuple-element.36), channel_id=1, source_target_pairs={{0,1},{1,0},{2,3},{3,2},{4,5},{5,4},{6,7},{7,6},{8,9},{9,8},{10,11... | collective-permute-start | bytes 638984 | tf_op jit(solution)/shard_map/ppermute | solution.py:612
  40.3 13.0 %collective-permute-start.6 = (bf16[32,5632]{1,0:T(8,128)(2,1)S(1)}, bf16[32,5632]{1,0:T(8,128)(2,1)S(1)}, u32[]{:S(2)}, u32[]{:S(2)}) collective-permute-start(bf16[32,5632]{1,0:T(8,128)(2,1)S(1)} %get-tuple-element.32), channel_id=1, source_target_pairs={{0,1},{1,0},{2,3},{3,2},{4,5},{5,4},{6,7},{7,6},{8,9},{9,8},{10,11... | collective-permute-start | bytes 1081352 | tf_op jit(solution)/shard_map/ppermute | solution.py:612

commit v3 on v2

--- a/solution.py
+++ b/solution.py
@@ -33,8 +33,10 @@
         self.inp = tuple(size + TILE for size in self.out)
         self.rows = up_to(self.win[1], 8)
         self.lane = 0
-        self.start = 0
-        self.span = up_to(self.full[0] * self.inp[1], LANES)
+        self.start = self.flat = 0
+        self.sent_rows = up_to(self.full[1], 8)
+        self.span = up_to(self.full[0] * self.sent_rows, LANES)
+        self.sent = up_to(self.low + self.high + REACH, 4)
 
 
 def levels_of(block):
@@ -44,6 +46,7 @@
         level.lane = lane
         lane += level.win[2]
     levels[3].start = levels[2].span
+    levels[3].flat = levels[2].full[0] * levels[2].inp[1]
     assert lane <= LANES and block[2] == LANES
     assert all(level.n[d] % 8 == 0 for level in levels for d in range(3))
     return levels
@@ -107,8 +110,8 @@
 
 
 def send_lanes(level):
-    up, down = np.zeros((SLAB, LANES)), np.zeros((SLAB, LANES))
-    for j in range(SLAB):
+    up, down = np.zeros((level.sent, LANES)), np.zeros((level.sent, LANES))
+    for j in range(level.sent):
         s = level.n[2] - REACH + j
         if s < level.win[2]:
             up[j, own_lane(level, s - level.low)] = 1
@@ -118,8 +121,8 @@
 
 
 def place_lanes(level):
-    from_prev, from_next = np.zeros((SLAB, LANES)), np.zeros((SLAB, LANES))
-    for j in range(SLAB):
+    from_prev, from_next = np.zeros((level.sent, LANES)), np.zeros((level.sent, LANES))
+    for j in range(level.sent):
         if level.n[2] - REACH + j < level.win[2]:
             from_prev[j, (level.lane + j) % LANES] = 1
         at = j + REACH + level.n[2]
@@ -366,8 +369,8 @@
 
 
 def lanes_kernel(levels, table, x_ref, prev_ref, next_ref, far_prev_ref, *refs):
-    far_next_ref = far_prev_ref if len(refs) == 5 else refs[0]
-    table_ref, flat_refs, slab_refs = refs[-5], refs[-4:-2], refs[-2:]
+    far_next_ref = far_prev_ref if len(refs) == 8 else refs[0]
+    table_ref, flat_refs, slab_refs, packed_refs = refs[-8], refs[-7:-5], refs[-5:-3], refs[-3:]
 
     def block_of(ref, block):
         return ref[block * SLAB : (block + 1) * SLAB].astype(F32)
@@ -381,7 +384,7 @@
 
     for level, mask in zip(levels[1:], lane_masks(levels)):
         blocks, step = level.inp[1] // 8, level.n[1] // 8
-        flat_ref = flat_refs[level.index > 1]
+        flat_ref, packed_ref = flat_refs[level.index > 1], packed_refs[level.index - 1]
         for at in range(level.full[0]):
             own = x_ref[plane_at(levels, level, at, "full")]
             slabs = [received(prev_ref, at, level), received(next_ref, at, level)]
@@ -398,24 +401,25 @@
                         terms.append(slab[8 * place : 8 * place + 8])
                 parts.append(total(terms) if terms else jnp.zeros((8, LANES), F32))
             value = jnp.where(mask, jnp.concatenate(parts, 0), 0.0)
-            first = level.start + at * level.inp[1]
+            first = level.flat + at * level.inp[1]
             flat_ref[first : first + level.inp[1]] = value
-        used = level.start + level.full[0] * level.inp[1]
-        last = level.start + level.span
-        if used < last:
-            flat_ref[used:last] = jnp.zeros((last - used, LANES), F32)
+            sent = level.sent_rows
+            packed_ref[at * sent : (at + 1) * sent] = value[:sent]
+        used = level.full[0] * level.sent_rows
+        if used < level.span:
+            packed_ref[used:] = jnp.zeros((level.span - used, LANES), F32)
     shift = levels[2].span + levels[3].span
-    for level in levels[1:]:
-        flat_ref, slab_ref = flat_refs[level.index > 1], slab_refs[level.index > 1]
+    for level, packed_ref in zip(levels[1:], packed_refs):
+        slab_ref = slab_refs[level.index > 1]
         send = table.get(table_ref, "send", level.index)
-        for first in range(level.start, level.start + level.span, 512):
-            stop = min(first + 512, level.start + level.span)
-            high, rest = halves_of(flat_ref[first:stop])
-            slab_ref[:, first:stop] = dot(send, high.astype(BF16), ((1,), (1,))).astype(BF16)
+        for first in range(0, level.span, 512):
+            stop = min(first + 512, level.span)
+            high, rest = halves_of(packed_ref[first:stop])
+            where = slice(level.start + first, level.start + stop)
+            slab_ref[:, where] = dot(send, high.astype(BF16), ((1,), (1,))).astype(BF16)
             if level.index > 1:
-                slab_ref[:, first + shift : stop + shift] = dot(
-                    send, rest.astype(BF16), ((1,), (1,))
-                ).astype(BF16)
+                where = slice(where.start + shift, where.stop + shift)
+                slab_ref[:, where] = dot(send, rest.astype(BF16), ((1,), (1,))).astype(BF16)
 
 
 def halo_kernel(wide_ref, out_ref):
@@ -492,18 +496,21 @@
 
 def level_passes(levels, level, table, flat_ref, slab_ref, lanes_ref, band_ref, table_ref, first_ref, second_ref, sum_ref):
     shift = levels[2].span + levels[3].span
-    rows, step = level.inp[1], 4
+    rows, sent, step = level.inp[1], level.sent_rows, 16
     first_lane, _ = lane_rows(level)
     place = table.get(table_ref, "place", level.index)
     for plane in range(0, level.full[0], step):
         count = min(step, level.full[0] - plane)
-        if (count * rows) % LANES:
-            count += 1
-        start, stop = level.start + plane * rows, level.start + (plane + count) * rows
+        start = level.start + plane * sent
+        stop = start + up_to(count * sent, LANES)
         slab = slab_ref[:, start:stop]
         if level.index > 1:
             slab = jnp.concatenate([slab, slab_ref[:, start + shift : stop + shift]], 0)
-        value = flat_ref[start:stop] + dot(slab, place, ((0,), (0,)))
+        extra = dot(slab, place, ((0,), (0,)))[: count * sent].reshape(count, sent, LANES)
+        if sent < rows:
+            extra = jnp.concatenate([extra, jnp.zeros((count, rows - sent, LANES), F32)], 1)
+        first = level.flat + plane * rows
+        value = flat_ref[first : first + count * rows] + extra.reshape(count * rows, LANES)
         result = dot(value.astype(BF16), lanes_ref[first_lane : first_lane + LANES])
         first_ref[plane : plane + count] = result.astype(BF16).reshape(count, rows, 4 * LANES)
     rest = level.inp[0] - plane - count
@@ -522,7 +529,7 @@
 
 
 def coarse_kernel(levels, table, flat_ref, slab_ref, lanes_ref, band_ref, table_ref, middle_ref, fine_ref, *refs):
-    out_ref, first_refs, second_refs, sum_refs = refs[0], refs[1:3], refs[3:5], refs[5:8]
+    out_hbm, first_refs, second_refs, sum_refs, out_ref, sems = refs[0], refs[1:3], refs[3:5], refs[5:8], refs[8], refs[9]
     for level in (levels[3], levels[2]):
         which = level.index - 2
         level_passes(
@@ -564,12 +571,17 @@
 
     stretch(levels[0], levels[1], sum_refs[0])
 
-    @pl.loop(0, levels[0].n[0] // 8)
-    def _(group):
-        def emit(at, value):
-            out_ref[at] = (fine_ref[at] + value).astype(BF16)
-
-        prolong(levels[0], levels[1], [4 * group + k for k in range(4)], sum_refs[0], emit)
+    def emit_fine(at, value):
+        out_ref[at] = (fine_ref[at] + value).astype(BF16)
+
+    copies = []
+    for group in range(levels[0].n[0] // 8):
+        prolong(levels[0], levels[1], [4 * group + k for k in range(4)], sum_refs[0], emit_fine)
+        where = slice(8 * group, 8 * group + 8)
+        copies.append(pltpu.make_async_copy(out_ref.at[where], out_hbm.at[where], sems.at[group]))
+        copies[-1].start()
+    for copy in copies:
+        copy.wait()
 
 
 def make_table(levels):
@@ -587,11 +599,11 @@
     first_ref[...] = charges_ref[:REACH]
 
 
-def call(kernel, out_shape, args, scratch=(), spaces={}, flops=0, limit=12):
+def call(kernel, out_shape, args, scratch=(), spaces={}, out_space=pltpu.VMEM, flops=0, limit=12):
     specs = [pl.BlockSpec(memory_space=spaces.get(i, pltpu.VMEM)) for i in range(len(args))]
     single = not isinstance(out_shape, (list, tuple))
     outs = [out_shape] if single else list(out_shape)
-    out_specs = [pl.BlockSpec(memory_space=pltpu.VMEM) for _ in outs]
+    out_specs = [pl.BlockSpec(memory_space=out_space) for _ in outs]
     return pl.pallas_call(
         kernel,
         out_shape=out_shape,
@@ -688,12 +700,17 @@
     )
     halo = z_pair(sides, "gz")
 
-    spans = (coarse[0].span, coarse[1].span + coarse[2].span)
+    flat_rows = [lv.full[0] * lv.inp[1] for lv in coarse]
+    slab_shapes = [
+        (2 * coarse[0].sent, coarse[0].span),
+        (2 * coarse[1].sent, 2 * (coarse[1].span + coarse[2].span)),
+    ]
     *flats, slab_one, slab_two = call(
         functools.partial(lanes_kernel, levels, table),
-        [shape((span, LANES), F32) for span in spans]
-        + [shape((2 * SLAB, count), BF16) for count in (spans[0], 2 * spans[1])],
+        [shape((count, LANES), F32) for count in (flat_rows[0], flat_rows[1] + flat_rows[2])]
+        + [shape(sizes, BF16) for sizes in slab_shapes],
         [r, m_prev, m_next, *far, table_array],
+        scratch=[pltpu.VMEM((lv.span, LANES), F32) for lv in coarse],
         flops=1 << 26,
     )
     slab_one = z_pair(slab_one, "gz")
@@ -729,7 +746,10 @@
         functools.partial(coarse_kernel, levels, table),
         shape(charges.shape, BF16),
         [flats[1], slab_two, lanes, band, table_array, middle, fine],
-        scratch=scratch(coarse[1:]) + [pltpu.VMEM((*lv.out, LANES), F32) for lv in coarse],
+        scratch=scratch(coarse[1:])
+        + [pltpu.VMEM((*lv.out, LANES), F32) for lv in coarse]
+        + [pltpu.VMEM(charges.shape, BF16), pltpu.SemaphoreType.DMA((charges.shape[0] // 8,))],
+        out_space=pl.ANY,
         flops=1 << 30,
         limit=16,
     )

time: 61.2 us -> 55.8 us (0.912)
  Pallas kernels: 27 us -> 22.2 us
  waiting for transfers between devices: 15.9 us -> 15.1 us
    pallas_call x9, Pallas kernels: 27 us -> 22.2 us  [call(): pl.pallas_call(kernel, out_shape=out_shape, in_specs=specs, out_specs=out...]
    ppermute x13, waiting for transfers between devices: 15.9 us -> 15.1 us  [shifted(): lax.ppermute(value, axis, [(i, (i + by) % count) for i in range(count)])]
  transfers between devices with their start and end apart: 13 -> 13, of which waited for: 5 -> 4; matrix products, arithmetic and copies ran while one was open for 0% -> 0% of each run, Pallas kernels for 32% -> 32%
where the time goes in v3:
time: 55.8 us; the launch traced here: 55.6 us
  Pallas kernels  22.2 us (40%)
  starting transfers between devices  16.5 us (30%)
  waiting for transfers between devices  15.1 us (27%)
  local copies, waits for them, and re-layouts  1.29 us (2%)
    pallas_call x9, Pallas kernels, call(): pl.pallas_call(kernel, out_shape=out_shape, in_specs=specs, out_specs=out...  22.2 us
    ppermute x13, starting transfers between devices, shifted(): lax.ppermute(value, axis, [(i, (i + by) % count) for i in range(count)])  16.5 us
    ppermute x13, waiting for transfers between devices, shifted(): lax.ppermute(value, axis, [(i, (i + by) % count) for i in range(count)])  15.1 us
    unnamed x8, local copies, waits for them, and re-layouts  1.24 us
  transfers between devices with their start and end apart: 13, of which 4 were waited for; matrix products, arithmetic and copies ran while one was open for 0% of the time, Pallas kernels for 32%

profile of v3, /device:TPU:0, one launch (start us, length us, event | category | flops | bytes accessed | tf_op | source)
XLA Modules:
  0.0 55.6 jit_solution(12936336323423836637)
XLA Ops:
  0.0 0.0 copy-start
  0.0 1.2 %copy-done = bf16[64,64,128]{2,1,0:T(8,128)(2,1)S(1)} copy-done((bf16[64,64,128]{2,1,0:T(8,128)(2,1)S(1)}, bf16[64,64,128]{2,1,0:T(8,128)(2,1)}, u32[]{:S(2)}) %copy-start) | copy-done | bytes 1048600
  1.2 3.1 %collective-permute-start.8 = (bf16[8,64,128]{2,1,0:T(8,128)(2,1)S(1)}, bf16[8,64,128]{2,1,0:T(8,128)(2,1)S(1)}, u32[]{:S(2)}, u32[]{:S(2)}) collective-permute-start(bf16[8,64,128]{2,1,0:T(8,128)(2,1)S(1)} %get-tuple-element.37), channel_id=1, source_target_pairs={{0,8},{8,16},{16,24},{24,0},{1,9},{9,17},{17,25},{25,1},{2,10},{10... | collective-permute-start | bytes 393224 | tf_op jit(solution)/shard_map/ppermute | solution.py:624
  4.4 2.1 %collective-permute-start.9 = (bf16[8,64,128]{2,1,0:T(8,128)(2,1)S(1)}, bf16[8,64,128]{2,1,0:T(8,128)(2,1)S(1)}, u32[]{:S(2)}, u32[]{:S(2)}) collective-permute-start(bf16[8,64,128]{2,1,0:T(8,128)(2,1)S(1)} %get-tuple-element.38), channel_id=1, source_target_pairs={{0,24},{8,0},{16,8},{24,16},{1,25},{9,1},{17,9},{25,17},{2,26},{10... | collective-permute-start | bytes 393224 | tf_op jit(solution)/shard_map/ppermute | solution.py:624
  6.5 0.0 copy-start.1
  6.5 4.2 %collective-permute-done.8 = bf16[8,64,128]{2,1,0:T(8,128)(2,1)S(1)} collective-permute-done((bf16[8,64,128]{2,1,0:T(8,128)(2,1)S(1)}, bf16[8,64,128]{2,1,0:T(8,128)(2,1)S(1)}, u32[]{:S(2)}, u32[]{:S(2)}) %collective-permute-start.8) | collective-permute-done | bytes 131104 | tf_op jit(solution)/shard_map/ppermute | solution.py:624
  10.7 1.4 %collective-permute-done.9 = bf16[8,64,128]{2,1,0:T(8,128)(2,1)S(1)} collective-permute-done((bf16[8,64,128]{2,1,0:T(8,128)(2,1)S(1)}, bf16[8,64,128]{2,1,0:T(8,128)(2,1)S(1)}, u32[]{:S(2)}, u32[]{:S(2)}) %collective-permute-start.9) | collective-permute-done | bytes 131104 | tf_op jit(solution)/shard_map/ppermute | solution.py:624
  12.2 0.6 %collective-permute-start.11 = (bf16[80,8,128]{2,1,0:T(8,128)(2,1)S(1)}, bf16[80,8,128]{2,1,0:T(8,128)(2,1)S(1)}, u32[]{:S(2)}, u32[]{:S(2)}) collective-permute-start(bf16[80,8,128]{2,1,0:T(8,128)(2,1)S(1)} %pad_maximum_fusion.2), channel_id=1, source_target_pairs={{0,6},{2,0},{4,2},{6,4},{1,7},{3,1},{5,3},{7,5},{8,14},{10,8},{12,... | collective-permute-start | bytes 491528 | tf_op jit(solution)/shard_map/ppermute | solution.py:624
  12.8 0.1 collective-permute-start.10
  12.8 3.0 %shard_map.37 = (f32[2112,128]{1,0:T(8,128)S(1)}, bf16[624,128]{1,0:T(8,128)(2,1)S(1)}, bf16[624,128]{1,0:T(8,128)(2,1)S(1)}, f32[3,16,128]{2,1,0:T(8,128)S(1)}) custom-call(bf16[64,64,128]{2,1,0:T(8,128)(2,1)S(1)} %copy-done), custom_call_target="tpu_custom_call" | custom-call | flops 134217728 | bytes 1048576 | tf_op jit(solution)/shard_map/pallas_call | solution.py:607
  15.8 1.7 %collective-permute-start = (bf16[624,128]{1,0:T(8,128)(2,1)S(1)}, bf16[624,128]{1,0:T(8,128)(2,1)S(1)}, u32[]{:S(2)}, u32[]{:S(2)}) collective-permute-start(bf16[624,128]{1,0:T(8,128)(2,1)S(1)} %get-tuple-element.24), channel_id=1, source_target_pairs={{0,8},{8,16},{16,24},{24,0},{1,9},{9,17},{17,25},{25,1},{2,10},{10... | collective-permute-start | bytes 479240 | tf_op jit(solution)/shard_map/ppermute | solution.py:624
  17.5 2.1 %collective-permute-start.1 = (bf16[624,128]{1,0:T(8,128)(2,1)S(1)}, bf16[624,128]{1,0:T(8,128)(2,1)S(1)}, u32[]{:S(2)}, u32[]{:S(2)}) collective-permute-start(bf16[624,128]{1,0:T(8,128)(2,1)S(1)} %get-tuple-element.25), channel_id=1, source_target_pairs={{0,24},{8,0},{16,8},{24,16},{1,25},{9,1},{17,9},{25,17},{2,26},{10... | collective-permute-start | bytes 479240 | tf_op jit(solution)/shard_map/ppermute | solution.py:624
  19.7 0.0 collective-permute-start.2
  19.7 8.2 %collective-permute-done.2.far_prev_ref = f32[3,16,128]{2,1,0:T(8,128)S(1)} collective-permute-done((f32[3,16,128]{2,1,0:T(8,128)S(1)}, f32[3,16,128]{2,1,0:T(8,128)S(1)}, u32[]{:S(2)}, u32[]{:S(2)}) %collective-permute-start.2) | collective-permute-done | bytes 24608 | tf_op jit(solution)/shard_map/ppermute | solution.py:624
  27.9 0.0 collective-permute-done.prev_ref
  27.9 0.0 collective-permute-done.1.next_ref
  27.9 0.3 shard_map.38
  28.3 0.1 collective-permute-start.3
  28.3 1.7 %collective-permute-start.4 = (bf16[1008,128]{1,0:T(8,128)(2,1)S(1)}, bf16[1008,128]{1,0:T(8,128)(2,1)S(1)}, u32[]{:S(2)}, u32[]{:S(2)}) collective-permute-start(bf16[1008,128]{1,0:T(8,128)(2,1)S(1)} %get-tuple-element.29), channel_id=1, source_target_pairs={{0,6},{2,0},{4,2},{6,4},{1,7},{3,1},{5,3},{7,5},{8,14},{10,8},{12,... | collective-permute-start | bytes 774152 | tf_op jit(solution)/shard_map/ppermute | solution.py:624
  30.1 0.0 collective-permute-done.11
  30.1 0.0 collective-permute-done.10
  30.1 0.0 copy-done.1
  30.1 0.2 pad_maximum_fusion.wide_ref
  30.3 0.0 copy-start.3
  30.3 0.0 copy-start.2
  30.3 0.6 %shard_map.42 = bf16[16,6400]{1,0:T(8,128)(2,1)S(1)} custom-call(bf16[80,80,128]{2,1,0:T(8,128)(2,1)S(1)} %pad_maximum_fusion.wide_ref), custom_call_target="tpu_custom_call" | custom-call | flops 67108864 | bytes 1048576 | tf_op jit(solution)/shard_map/pallas_call | solution.py:607
  30.9 1.6 %collective-permute-start.12 = (bf16[16,6400]{1,0:T(8,128)(2,1)S(1)}, bf16[16,6400]{1,0:T(8,128)(2,1)S(1)}, u32[]{:S(2)}, u32[]{:S(2)}) collective-permute-start(bf16[16,6400]{1,0:T(8,128)(2,1)S(1)} %shard_map.42), channel_id=1, source_target_pairs={{0,1},{1,0},{2,3},{3,2},{4,5},{5,4},{6,7},{7,6},{8,9},{9,8},{10,11... | collective-permute-start | bytes 614408 | tf_op jit(solution)/shard_map/ppermute | solution.py:624
  32.4 1.4 %collective-permute-start.5 = (f32[5,16,128]{2,1,0:T(8,128)S(1)}, f32[5,16,128]{2,1,0:T(8,128)S(1)}, u32[]{:S(2)}, u32[]{:S(2)}) collective-permute-start(f32[5,16,128]{2,1,0:T(8,128)S(1)} %get-tuple-element.30), channel_id=1, source_target_pairs={{0,4},{2,6},{4,0},{6,2},{1,5},{3,7},{5,1},{7,3},{8,12},{10,14},{12... | collective-permute-start | bytes 122888 | tf_op jit(solution)/shard_map/ppermute | solution.py:624
  33.9 0.0 copy-done.3
  33.9 3.9 %shard_map.40 = (bf16[16,128,256]{2,1,0:T(8,128)(2,1)S(1)}, bf16[640,512]{1,0:T(8,128)(2,1)S(1)}) custom-call(f32[16,17]{1,0:T(8,128)S(1)} %bitcast.1), custom_call_target="tpu_custom_call" | custom-call | flops 67108864 | bytes 1048576 | tf_op jit(solution)/shard_map/pallas_call | solution.py:607
  37.8 0.0 collective-permute-done.5.far_prev_ref
  37.8 0.0 collective-permute-done.3.prev_ref
  37.8 0.0 collective-permute-done.4.next_ref
  37.8 0.0 copy-done.2
  37.8 0.9 %shard_map.39 = (f32[3264,128]{1,0:T(8,128)S(1)}, f32[2704,128]{1,0:T(8,128)S(1)}, bf16[24,2944]{1,0:T(8,128)(2,1)S(1)}, bf16[32,5120]{1,0:T(8,128)(2,1)S(1)}) custom-call(f32[3392,128]{1,0:T(8,128)S(1)} %get-tuple-element.27.x_ref, bf16[1008,128]{1,0:T(8,128)(2,1)S(1)} %collective-permute-done.3.prev_ref, ...), custom_call_target="tpu_custom_call" | custom-call | flops 67108864 | bytes 1048576 | tf_op jit(solution)/shard_map/pallas_call | solution.py:607
  38.7 1.5 %collective-permute-start.7 = (bf16[24,2944]{1,0:T(8,128)(2,1)S(1)}, bf16[24,2944]{1,0:T(8,128)(2,1)S(1)}, u32[]{:S(2)}, u32[]{:S(2)}) collective-permute-start(bf16[24,2944]{1,0:T(8,128)(2,1)S(1)} %get-tuple-element.36), channel_id=1, source_target_pairs={{0,1},{1,0},{2,3},{3,2},{4,5},{5,4},{6,7},{7,6},{8,9},{9,8},{10,11... | collective-permute-start | bytes 423944 | tf_op jit(solution)/shard_map/ppermute | solution.py:624
  40.2 0.6 %collective-permute-start.6 = (bf16[32,5120]{1,0:T(8,128)(2,1)S(1)}, bf16[32,5120]{1,0:T(8,128)(2,1)S(1)}, u32[]{:S(2)}, u32[]{:S(2)}) collective-permute-start(bf16[32,5120]{1,0:T(8,128)(2,1)S(1)} %get-tuple-element.32), channel_id=1, source_target_pairs={{0,1},{1,0},{2,3},{3,2},{4,5},{5,4},{6,7},{7,6},{8,9},{9,8},{10,11... | collective-permute-start | bytes 983048 | tf_op jit(solution)/shard_map/ppermute | solution.py:624
  40.8 0.0 collective-permute-done.12.halo_ref
  40.8 5.9 %shard_map.43.fine_ref = f32[64,64,128]{2,1,0:T(8,128)S(1)} custom-call(bf16[80,80,128]{2,1,0:T(8,128)(2,1)S(1)} %pad_maximum_fusion.wide_ref, bf16[16,6400]{1,0:T(8,128)(2,1)S(1)} %collective-permute-done.12.halo_ref, bf16[640,512]{1,0:T(8,128)(2,1)S(1)} %get-tuple-element.33.lanes_ref, bf16[16,128,256]{2,1,0:T(8,128)(2,1)S(1)} %get-tuple-element.34.band_ref), custom_call_target="tpu_custom_call" | custom-call | flops 4294967296 | bytes 1048576 | tf_op jit(solution)/shard_map/pallas_call | solution.py:607
  46.7 0.0 collective-permute-done.7.slab_ref
  46.7 3.0 %shard_map.44.middle_ref = f32[48,48,128]{2,1,0:T(8,128)S(1)} custom-call(f32[3264,128]{1,0:T(8,128)S(1)} %get-tuple-element.35.flat_ref, bf16[24,2944]{1,0:T(8,128)(2,1)S(1)} %collective-permute-done.7.slab_ref, bf16[640,512]{1,0:T(8,128)(2,1)S(1)} %get-tuple-element.33.lanes_ref, bf16[16,128,256]{2,1,0:T(8,128)(2,1)S(1)} %get-tuple-element.34.band_ref, ...), custom_call_target="tpu_custom_call" | custom-call | flops 2147483648 | bytes 1048576 | tf_op jit(solution)/shard_map/pallas_call | solution.py:607
  49.7 1.2 %collective-permute-done.6.slab_ref = bf16[32,5120]{1,0:T(8,128)(2,1)S(1)} collective-permute-done((bf16[32,5120]{1,0:T(8,128)(2,1)S(1)}, bf16[32,5120]{1,0:T(8,128)(2,1)S(1)}, u32[]{:S(2)}, u32[]{:S(2)}) %collective-permute-start.6) | collective-permute-done | bytes 327712 | tf_op jit(solution)/shard_map/ppermute | solution.py:624
  51.0 4.5 %shard_map.45 = bf16[64,64,128]{2,1,0:T(8,128)(2,1)} custom-call(f32[2704,128]{1,0:T(8,128)S(1)} %get-tuple-element.31.flat_ref, bf16[32,5120]{1,0:T(8,128)(2,1)S(1)} %collective-permute-done.6.slab_ref, bf16[640,512]{1,0:T(8,128)(2,1)S(1)} %get-tuple-element.33.lanes_ref, bf16[16,128,256]{2,1,0:T(8,128)(2,1)S(1)} %get-tuple-element.34.band_ref, ...), custom_call_target="tpu_custom_call" | custom-call | flops 1073741824 | bytes 1048576 | tf_op jit(solution)/shard_map/pallas_call | solution.py:607
  (6 shorter events, 0.1 us)
Async XLA Ops:
  0.0 1.2 %copy-start = (bf16[64,64,128]{2,1,0:T(8,128)(2,1)S(1)}, bf16[64,64,128]{2,1,0:T(8,128)(2,1)}, u32[]{:S(2)}) copy-start(bf16[64,64,128]{2,1,0:T(8,128)(2,1)} %charges_ref.3) | copy-start | bytes 3145732
  1.2 9.5 %collective-permute-start.8 = (bf16[8,64,128]{2,1,0:T(8,128)(2,1)S(1)}, bf16[8,64,128]{2,1,0:T(8,128)(2,1)S(1)}, u32[]{:S(2)}, u32[]{:S(2)}) collective-permute-start(bf16[8,64,128]{2,1,0:T(8,128)(2,1)S(1)} %get-tuple-element.37), channel_id=1, source_target_pairs={{0,8},{8,16},{16,24},{24,0},{1,9},{9,17},{17,25},{25,1},{2,10},{10... | collective-permute-start | bytes 393224 | tf_op jit(solution)/shard_map/ppermute | solution.py:624
  4.4 7.8 %collective-permute-start.9 = (bf16[8,64,128]{2,1,0:T(8,128)(2,1)S(1)}, bf16[8,64,128]{2,1,0:T(8,128)(2,1)S(1)}, u32[]{:S(2)}, u32[]{:S(2)}) collective-permute-start(bf16[8,64,128]{2,1,0:T(8,128)(2,1)S(1)} %get-tuple-element.38), channel_id=1, source_target_pairs={{0,24},{8,0},{16,8},{24,16},{1,25},{9,1},{17,9},{25,17},{2,26},{10... | collective-permute-start | bytes 393224 | tf_op jit(solution)/shard_map/ppermute | solution.py:624
  6.5 23.6 %copy-start.1 = (bf16[64,64,128]{2,1,0:T(8,128)(2,1)S(1)}, bf16[64,64,128]{2,1,0:T(8,128)(2,1)}, u32[]{:S(2)}) copy-start(bf16[64,64,128]{2,1,0:T(8,128)(2,1)} %charges_ref.3) | copy-start | bytes 3145732
  12.2 17.9 %collective-permute-start.11 = (bf16[80,8,128]{2,1,0:T(8,128)(2,1)S(1)}, bf16[80,8,128]{2,1,0:T(8,128)(2,1)S(1)}, u32[]{:S(2)}, u32[]{:S(2)}) collective-permute-start(bf16[80,8,128]{2,1,0:T(8,128)(2,1)S(1)} %pad_maximum_fusion.2), channel_id=1, source_target_pairs={{0,6},{2,0},{4,2},{6,4},{1,7},{3,1},{5,3},{7,5},{8,14},{10,8},{12,... | collective-permute-start | bytes 491528 | tf_op jit(solution)/shard_map/ppermute | solution.py:624
  12.8 17.3 %collective-permute-start.10 = (bf16[80,8,128]{2,1,0:T(8,128)(2,1)S(1)}, bf16[80,8,128]{2,1,0:T(8,128)(2,1)S(1)}, u32[]{:S(2)}, u32[]{:S(2)}) collective-permute-start(bf16[80,8,128]{2,1,0:T(8,128)(2,1)S(1)} %pad_maximum_fusion.1), channel_id=1, source_target_pairs={{0,2},{2,4},{4,6},{6,0},{1,3},{3,5},{5,7},{7,1},{8,10},{10,12},{12... | collective-permute-start | bytes 491528 | tf_op jit(solution)/shard_map/ppermute | solution.py:624
  15.8 12.1 %collective-permute-start = (bf16[624,128]{1,0:T(8,128)(2,1)S(1)}, bf16[624,128]{1,0:T(8,128)(2,1)S(1)}, u32[]{:S(2)}, u32[]{:S(2)}) collective-permute-start(bf16[624,128]{1,0:T(8,128)(2,1)S(1)} %get-tuple-element.24), channel_id=1, source_target_pairs={{0,8},{8,16},{16,24},{24,0},{1,9},{9,17},{17,25},{25,1},{2,10},{10... | collective-permute-start | bytes 479240 | tf_op jit(solution)/shard_map/ppermute | solution.py:624
  17.5 10.4 %collective-permute-start.1 = (bf16[624,128]{1,0:T(8,128)(2,1)S(1)}, bf16[624,128]{1,0:T(8,128)(2,1)S(1)}, u32[]{:S(2)}, u32[]{:S(2)}) collective-permute-start(bf16[624,128]{1,0:T(8,128)(2,1)S(1)} %get-tuple-element.25), channel_id=1, source_target_pairs={{0,24},{8,0},{16,8},{24,16},{1,25},{9,1},{17,9},{25,17},{2,26},{10... | collective-permute-start | bytes 479240 | tf_op jit(solution)/shard_map/ppermute | solution.py:624
  19.7 8.2 %collective-permute-start.2 = (f32[3,16,128]{2,1,0:T(8,128)S(1)}, f32[3,16,128]{2,1,0:T(8,128)S(1)}, u32[]{:S(2)}, u32[]{:S(2)}) collective-permute-start(f32[3,16,128]{2,1,0:T(8,128)S(1)} %get-tuple-element.26), channel_id=1, source_target_pairs={{0,16},{8,24},{16,0},{24,8},{1,17},{9,25},{17,1},{25,9},{2,18},{10... | collective-permute-start | bytes 73736 | tf_op jit(solution)/shard_map/ppermute | solution.py:624
  28.3 9.5 %collective-permute-start.3 = (bf16[1008,128]{1,0:T(8,128)(2,1)S(1)}, bf16[1008,128]{1,0:T(8,128)(2,1)S(1)}, u32[]{:S(2)}, u32[]{:S(2)}) collective-permute-start(bf16[1008,128]{1,0:T(8,128)(2,1)S(1)} %get-tuple-element.28), channel_id=1, source_target_pairs={{0,2},{2,4},{4,6},{6,0},{1,3},{3,5},{5,7},{7,1},{8,10},{10,12},{12... | collective-permute-start | bytes 774152 | tf_op jit(solution)/shard_map/ppermute | solution.py:624
  28.3 9.5 %collective-permute-start.4 = (bf16[1008,128]{1,0:T(8,128)(2,1)S(1)}, bf16[1008,128]{1,0:T(8,128)(2,1)S(1)}, u32[]{:S(2)}, u32[]{:S(2)}) collective-permute-start(bf16[1008,128]{1,0:T(8,128)(2,1)S(1)} %get-tuple-element.29), channel_id=1, source_target_pairs={{0,6},{2,0},{4,2},{6,4},{1,7},{3,1},{5,3},{7,5},{8,14},{10,8},{12,... | collective-permute-start | bytes 774152 | tf_op jit(solution)/shard_map/ppermute | solution.py:624
  30.3 3.6 %copy-start.3 = (f32[4,4,17]{2,1,0:T(4,128)S(1)}, f32[4,4,17]{2,1,0:T(4,128)}, u32[]{:S(2)}) copy-start(f32[4,4,17]{2,1,0:T(4,128)} %param.4) | copy-start | bytes 3268
  30.3 7.6 %copy-start.2 = (bf16[1168,128]{1,0:T(8,128)(2,1)S(1)}, bf16[1168,128]{1,0:T(8,128)(2,1)}, u32[]{:S(2)}) copy-start(bf16[1168,128]{1,0:T(8,128)(2,1)} %constant.2.clone.refs_0_.table_ref) | copy-start | bytes 897028
  30.9 9.9 %collective-permute-start.12 = (bf16[16,6400]{1,0:T(8,128)(2,1)S(1)}, bf16[16,6400]{1,0:T(8,128)(2,1)S(1)}, u32[]{:S(2)}, u32[]{:S(2)}) collective-permute-start(bf16[16,6400]{1,0:T(8,128)(2,1)S(1)} %shard_map.42), channel_id=1, source_target_pairs={{0,1},{1,0},{2,3},{3,2},{4,5},{5,4},{6,7},{7,6},{8,9},{9,8},{10,11... | collective-permute-start | bytes 614408 | tf_op jit(solution)/shard_map/ppermute | solution.py:624
  32.4 5.4 %collective-permute-start.5 = (f32[5,16,128]{2,1,0:T(8,128)S(1)}, f32[5,16,128]{2,1,0:T(8,128)S(1)}, u32[]{:S(2)}, u32[]{:S(2)}) collective-permute-start(f32[5,16,128]{2,1,0:T(8,128)S(1)} %get-tuple-element.30), channel_id=1, source_target_pairs={{0,4},{2,6},{4,0},{6,2},{1,5},{3,7},{5,1},{7,3},{8,12},{10,14},{12... | collective-permute-start | bytes 122888 | tf_op jit(solution)/shard_map/ppermute | solution.py:624
  38.7 8.0 %collective-permute-start.7 = (bf16[24,2944]{1,0:T(8,128)(2,1)S(1)}, bf16[24,2944]{1,0:T(8,128)(2,1)S(1)}, u32[]{:S(2)}, u32[]{:S(2)}) collective-permute-start(bf16[24,2944]{1,0:T(8,128)(2,1)S(1)} %get-tuple-element.36), channel_id=1, source_target_pairs={{0,1},{1,0},{2,3},{3,2},{4,5},{5,4},{6,7},{7,6},{8,9},{9,8},{10,11... | collective-permute-start | bytes 423944 | tf_op jit(solution)/shard_map/ppermute | solution.py:624
  40.2 10.8 %collective-permute-start.6 = (bf16[32,5120]{1,0:T(8,128)(2,1)S(1)}, bf16[32,5120]{1,0:T(8,128)(2,1)S(1)}, u32[]{:S(2)}, u32[]{:S(2)}) collective-permute-start(bf16[32,5120]{1,0:T(8,128)(2,1)S(1)} %get-tuple-element.32), channel_id=1, source_target_pairs={{0,1},{1,0},{2,3},{3,2},{4,5},{5,4},{6,7},{7,6},{8,9},{9,8},{10,11... | collective-permute-start | bytes 983048 | tf_op jit(solution)/shard_map/ppermute | solution.py:624

commit v4 on v3

--- a/solution.py
+++ b/solution.py
@@ -368,9 +368,10 @@
     pack_far(levels, far_ref, coarsest)
 
 
-def lanes_kernel(levels, table, x_ref, prev_ref, next_ref, far_prev_ref, *refs):
-    far_next_ref = far_prev_ref if len(refs) == 8 else refs[0]
-    table_ref, flat_refs, slab_refs, packed_refs = refs[-8], refs[-7:-5], refs[-5:-3], refs[-3:]
+def lanes_kernel(levels, some, table, x_ref, prev_ref, next_ref, table_ref, *refs):
+    far_refs, (flat_ref, slab_ref) = refs[: -2 - len(some)], refs[-2 - len(some) : -len(some)]
+    packed_refs = refs[-len(some) :]
+    masks = dict(zip(range(1, 4), lane_masks(levels)))
 
     def block_of(ref, block):
         return ref[block * SLAB : (block + 1) * SLAB].astype(F32)
@@ -382,14 +383,14 @@
         block, lanes = rest_block(levels, at)
         return high + turned(block_of(ref, block), LANES - lanes)
 
-    for level, mask in zip(levels[1:], lane_masks(levels)):
+    for level, packed_ref in zip(some, packed_refs):
+        mask = masks[level.index]
         blocks, step = level.inp[1] // 8, level.n[1] // 8
-        flat_ref, packed_ref = flat_refs[level.index > 1], packed_refs[level.index - 1]
         for at in range(level.full[0]):
             own = x_ref[plane_at(levels, level, at, "full")]
             slabs = [received(prev_ref, at, level), received(next_ref, at, level)]
             if level.index == 3:
-                slabs += [unpack_far(levels, ref, at) for ref in (far_prev_ref, far_next_ref)]
+                slabs += [unpack_far(levels, ref, at) for ref in (far_refs[0], far_refs[-1])]
             parts = []
             for block in range(blocks):
                 terms = []
@@ -409,8 +410,7 @@
         if used < level.span:
             packed_ref[used:] = jnp.zeros((level.span - used, LANES), F32)
     shift = levels[2].span + levels[3].span
-    for level, packed_ref in zip(levels[1:], packed_refs):
-        slab_ref = slab_refs[level.index > 1]
+    for level, packed_ref in zip(some, packed_refs):
         send = table.get(table_ref, "send", level.index)
         for first in range(0, level.span, 512):
             stop = min(first + 512, level.span)
@@ -480,13 +480,12 @@
     lane = lax.broadcasted_iota(jnp.int32, (2 * REACH, LANES), 1)
     place = jnp.where(lane == row, 1.0, 0.0).astype(BF16)
 
-    @pl.loop(0, level.inp[0] // step)
-    def _(chunk):
-        where = pl.ds(pl.multiple_of(chunk * step * rows, LANES), step * rows)
+    for chunk in range(level.inp[0] // step):
+        where = slice(chunk * step * rows, (chunk + 1) * step * rows)
         sides = dot(halo_ref[:, where], place, ((0,), (0,))).astype(BF16)
-        here = wide_ref[pl.ds(chunk * step, step)].reshape(step * rows, LANES)
+        here = wide_ref[chunk * step : (chunk + 1) * step].reshape(step * rows, LANES)
         result = dot(jnp.concatenate([here, sides], 1), lanes_ref[: 2 * LANES])
-        first_ref[pl.ds(chunk * step, step)] = result.astype(BF16).reshape(step, rows, 4 * LANES)
+        first_ref[chunk * step : (chunk + 1) * step] = result.astype(BF16).reshape(step, rows, 4 * LANES)
 
     def put(block, pair, value):
         out_ref[TILE * block : TILE * (block + 1), slice(pair * 16, pair * 16 + 16)] = value
@@ -705,14 +704,20 @@
         (2 * coarse[0].sent, coarse[0].span),
         (2 * coarse[1].sent, 2 * (coarse[1].span + coarse[2].span)),
     ]
-    *flats, slab_one, slab_two = call(
-        functools.partial(lanes_kernel, levels, table),
-        [shape((count, LANES), F32) for count in (flat_rows[0], flat_rows[1] + flat_rows[2])]
-        + [shape(sizes, BF16) for sizes in slab_shapes],
-        [r, m_prev, m_next, *far, table_array],
-        scratch=[pltpu.VMEM((lv.span, LANES), F32) for lv in coarse],
-        flops=1 << 26,
-    )
+    groups = (coarse[:1], coarse[1:])
+    (flat_one, slab_one), (flat_two, slab_two) = [
+        call(
+            functools.partial(lanes_kernel, levels, some, table),
+            [shape((count, LANES), F32), shape(sizes, BF16)],
+            [r, m_prev, m_next, table_array, *extra],
+            scratch=[pltpu.VMEM((lv.span, LANES), F32) for lv in some],
+            flops=1 << 26,
+        )
+        for some, count, sizes, extra in zip(
+            groups, (flat_rows[0], flat_rows[1] + flat_rows[2]), slab_shapes, ([], far)
+        )
+    ]
+    flats = (flat_one, flat_two)
     slab_one = z_pair(slab_one, "gz")
     slab_two = z_pair(slab_two, "gz")
 

time: 55.8 us -> 55.4 us (level)
  Pallas kernels: 22.2 us -> 21.5 us
    pallas_call x9 -> x10, Pallas kernels: 22.2 us -> 21.5 us  [call(): pl.pallas_call(kernel, out_shape=out_shape, in_specs=specs, out_specs=out...]
  transfers between devices with their start and end apart: 13 -> 13, of which waited for: 4 -> 4; matrix products, arithmetic and copies ran while one was open for 0% -> 0% of each run, Pallas kernels for 32% -> 31%
where the time goes in v4:
time: 55.4 us; the launch traced here: 55.2 us
  Pallas kernels  21.5 us (39%)
  starting transfers between devices  16.6 us (30%)
  waiting for transfers between devices  15.3 us (28%)
  local copies, waits for them, and re-layouts  1.29 us (2%)
    pallas_call x10, Pallas kernels, call(): pl.pallas_call(kernel, out_shape=out_shape, in_specs=specs, out_specs=out...  21.5 us
    ppermute x13, starting transfers between devices, shifted(): lax.ppermute(value, axis, [(i, (i + by) % count) for i in range(count)])  16.6 us
    ppermute x13, waiting for transfers between devices, shifted(): lax.ppermute(value, axis, [(i, (i + by) % count) for i in range(count)])  15.3 us
    unnamed x8, local copies, waits for them, and re-layouts  1.24 us
  transfers between devices with their start and end apart: 13, of which 4 were waited for; matrix products, arithmetic and copies ran while one was open for 0% of the time, Pallas kernels for 31%

profile of v4, /device:TPU:0, one launch (start us, length us, event | category | flops | bytes accessed | tf_op | source)
XLA Modules:
  0.0 55.2 jit_solution(10154791693658275300)
XLA Ops:
  0.0 0.0 copy-start
  0.0 1.2 %copy-done = bf16[64,64,128]{2,1,0:T(8,128)(2,1)S(1)} copy-done((bf16[64,64,128]{2,1,0:T(8,128)(2,1)S(1)}, bf16[64,64,128]{2,1,0:T(8,128)(2,1)}, u32[]{:S(2)}) %copy-start) | copy-done | bytes 1048600
  1.2 3.1 %collective-permute-start.8 = (bf16[8,64,128]{2,1,0:T(8,128)(2,1)S(1)}, bf16[8,64,128]{2,1,0:T(8,128)(2,1)S(1)}, u32[]{:S(2)}, u32[]{:S(2)}) collective-permute-start(bf16[8,64,128]{2,1,0:T(8,128)(2,1)S(1)} %get-tuple-element.37), channel_id=1, source_target_pairs={{0,8},{8,16},{16,24},{24,0},{1,9},{9,17},{17,25},{25,1},{2,10},{10... | collective-permute-start | bytes 393224 | tf_op jit(solution)/shard_map/ppermute | solution.py:623
  4.4 2.1 %collective-permute-start.9 = (bf16[8,64,128]{2,1,0:T(8,128)(2,1)S(1)}, bf16[8,64,128]{2,1,0:T(8,128)(2,1)S(1)}, u32[]{:S(2)}, u32[]{:S(2)}) collective-permute-start(bf16[8,64,128]{2,1,0:T(8,128)(2,1)S(1)} %get-tuple-element.38), channel_id=1, source_target_pairs={{0,24},{8,0},{16,8},{24,16},{1,25},{9,1},{17,9},{25,17},{2,26},{10... | collective-permute-start | bytes 393224 | tf_op jit(solution)/shard_map/ppermute | solution.py:623
  6.5 0.0 copy-start.1
  6.5 4.2 %collective-permute-done.8 = bf16[8,64,128]{2,1,0:T(8,128)(2,1)S(1)} collective-permute-done((bf16[8,64,128]{2,1,0:T(8,128)(2,1)S(1)}, bf16[8,64,128]{2,1,0:T(8,128)(2,1)S(1)}, u32[]{:S(2)}, u32[]{:S(2)}) %collective-permute-start.8) | collective-permute-done | bytes 131104 | tf_op jit(solution)/shard_map/ppermute | solution.py:623
  10.7 1.4 %collective-permute-done.9 = bf16[8,64,128]{2,1,0:T(8,128)(2,1)S(1)} collective-permute-done((bf16[8,64,128]{2,1,0:T(8,128)(2,1)S(1)}, bf16[8,64,128]{2,1,0:T(8,128)(2,1)S(1)}, u32[]{:S(2)}, u32[]{:S(2)}) %collective-permute-start.9) | collective-permute-done | bytes 131104 | tf_op jit(solution)/shard_map/ppermute | solution.py:623
  12.2 0.6 %collective-permute-start.11 = (bf16[80,8,128]{2,1,0:T(8,128)(2,1)S(1)}, bf16[80,8,128]{2,1,0:T(8,128)(2,1)S(1)}, u32[]{:S(2)}, u32[]{:S(2)}) collective-permute-start(bf16[80,8,128]{2,1,0:T(8,128)(2,1)S(1)} %pad_maximum_fusion.2), channel_id=1, source_target_pairs={{0,6},{2,0},{4,2},{6,4},{1,7},{3,1},{5,3},{7,5},{8,14},{10,8},{12,... | collective-permute-start | bytes 491528 | tf_op jit(solution)/shard_map/ppermute | solution.py:623
  12.8 0.1 collective-permute-start.10
  12.8 3.0 %shard_map.37 = (f32[2112,128]{1,0:T(8,128)S(1)}, bf16[624,128]{1,0:T(8,128)(2,1)S(1)}, bf16[624,128]{1,0:T(8,128)(2,1)S(1)}, f32[3,16,128]{2,1,0:T(8,128)S(1)}) custom-call(bf16[64,64,128]{2,1,0:T(8,128)(2,1)S(1)} %copy-done), custom_call_target="tpu_custom_call" | custom-call | flops 134217728 | bytes 1048576 | tf_op jit(solution)/shard_map/pallas_call | solution.py:606
  15.8 1.7 %collective-permute-start = (bf16[624,128]{1,0:T(8,128)(2,1)S(1)}, bf16[624,128]{1,0:T(8,128)(2,1)S(1)}, u32[]{:S(2)}, u32[]{:S(2)}) collective-permute-start(bf16[624,128]{1,0:T(8,128)(2,1)S(1)} %get-tuple-element.24), channel_id=1, source_target_pairs={{0,8},{8,16},{16,24},{24,0},{1,9},{9,17},{17,25},{25,1},{2,10},{10... | collective-permute-start | bytes 479240 | tf_op jit(solution)/shard_map/ppermute | solution.py:623
  17.5 2.1 %collective-permute-start.1 = (bf16[624,128]{1,0:T(8,128)(2,1)S(1)}, bf16[624,128]{1,0:T(8,128)(2,1)S(1)}, u32[]{:S(2)}, u32[]{:S(2)}) collective-permute-start(bf16[624,128]{1,0:T(8,128)(2,1)S(1)} %get-tuple-element.25), channel_id=1, source_target_pairs={{0,24},{8,0},{16,8},{24,16},{1,25},{9,1},{17,9},{25,17},{2,26},{10... | collective-permute-start | bytes 479240 | tf_op jit(solution)/shard_map/ppermute | solution.py:623
  19.7 0.0 collective-permute-start.2
  19.7 8.2 %collective-permute-done.2.far_prev_ref = f32[3,16,128]{2,1,0:T(8,128)S(1)} collective-permute-done((f32[3,16,128]{2,1,0:T(8,128)S(1)}, f32[3,16,128]{2,1,0:T(8,128)S(1)}, u32[]{:S(2)}, u32[]{:S(2)}) %collective-permute-start.2) | collective-permute-done | bytes 24608 | tf_op jit(solution)/shard_map/ppermute | solution.py:623
  27.9 0.0 collective-permute-done.prev_ref
  27.9 0.0 collective-permute-done.1.next_ref
  27.9 0.3 shard_map.38
  28.3 0.1 collective-permute-start.3
  28.3 1.7 %collective-permute-start.4 = (bf16[1008,128]{1,0:T(8,128)(2,1)S(1)}, bf16[1008,128]{1,0:T(8,128)(2,1)S(1)}, u32[]{:S(2)}, u32[]{:S(2)}) collective-permute-start(bf16[1008,128]{1,0:T(8,128)(2,1)S(1)} %get-tuple-element.29), channel_id=1, source_target_pairs={{0,6},{2,0},{4,2},{6,4},{1,7},{3,1},{5,3},{7,5},{8,14},{10,8},{12,... | collective-permute-start | bytes 774152 | tf_op jit(solution)/shard_map/ppermute | solution.py:623
  30.1 0.0 collective-permute-done.11
  30.1 0.0 collective-permute-done.10
  30.1 0.0 copy-done.1
  30.1 0.2 pad_maximum_fusion.wide_ref
  30.3 0.0 copy-start.3
  30.3 0.0 copy-start.2
  30.3 0.6 %shard_map.43 = bf16[16,6400]{1,0:T(8,128)(2,1)S(1)} custom-call(bf16[80,80,128]{2,1,0:T(8,128)(2,1)S(1)} %pad_maximum_fusion.wide_ref), custom_call_target="tpu_custom_call" | custom-call | flops 67108864 | bytes 1048576 | tf_op jit(solution)/shard_map/pallas_call | solution.py:606
  30.9 1.6 %collective-permute-start.12 = (bf16[16,6400]{1,0:T(8,128)(2,1)S(1)}, bf16[16,6400]{1,0:T(8,128)(2,1)S(1)}, u32[]{:S(2)}, u32[]{:S(2)}) collective-permute-start(bf16[16,6400]{1,0:T(8,128)(2,1)S(1)} %shard_map.43), channel_id=1, source_target_pairs={{0,1},{1,0},{2,3},{3,2},{4,5},{5,4},{6,7},{7,6},{8,9},{9,8},{10,11... | collective-permute-start | bytes 614408 | tf_op jit(solution)/shard_map/ppermute | solution.py:623
  32.4 1.4 %collective-permute-start.5 = (f32[5,16,128]{2,1,0:T(8,128)S(1)}, f32[5,16,128]{2,1,0:T(8,128)S(1)}, u32[]{:S(2)}, u32[]{:S(2)}) collective-permute-start(f32[5,16,128]{2,1,0:T(8,128)S(1)} %get-tuple-element.30), channel_id=1, source_target_pairs={{0,4},{2,6},{4,0},{6,2},{1,5},{3,7},{5,1},{7,3},{8,12},{10,14},{12... | collective-permute-start | bytes 122888 | tf_op jit(solution)/shard_map/ppermute | solution.py:623
  33.9 0.0 copy-done.3
  33.9 4.1 %shard_map.40 = (bf16[16,128,256]{2,1,0:T(8,128)(2,1)S(1)}, bf16[640,512]{1,0:T(8,128)(2,1)S(1)}) custom-call(f32[16,17]{1,0:T(8,128)S(1)} %bitcast.1), custom_call_target="tpu_custom_call" | custom-call | flops 67108864 | bytes 1048576 | tf_op jit(solution)/shard_map/pallas_call | solution.py:606
  38.0 0.0 collective-permute-done.3.prev_ref
  38.0 0.0 collective-permute-done.4.next_ref
  38.0 0.0 copy-done.2
  38.0 0.4 shard_map.41
  38.4 0.6 %collective-permute-start.7 = (bf16[24,2944]{1,0:T(8,128)(2,1)S(1)}, bf16[24,2944]{1,0:T(8,128)(2,1)S(1)}, u32[]{:S(2)}, u32[]{:S(2)}) collective-permute-start(bf16[24,2944]{1,0:T(8,128)(2,1)S(1)} %get-tuple-element.36), channel_id=1, source_target_pairs={{0,1},{1,0},{2,3},{3,2},{4,5},{5,4},{6,7},{7,6},{8,9},{9,8},{10,11... | collective-permute-start | bytes 423944 | tf_op jit(solution)/shard_map/ppermute | solution.py:623
  38.9 0.0 collective-permute-done.5.refs_0_
  38.9 0.6 %shard_map.39 = (f32[2704,128]{1,0:T(8,128)S(1)}, bf16[32,5120]{1,0:T(8,128)(2,1)S(1)}) custom-call(f32[3392,128]{1,0:T(8,128)S(1)} %get-tuple-element.27.x_ref, bf16[1008,128]{1,0:T(8,128)(2,1)S(1)} %collective-permute-done.3.prev_ref, bf16[1008,128]{1,0:T(8,128)(2,1)S(1)} %collective-permute-done.4.next_ref, bf16[1168,128]{1,0:T(8,128)(2,1)S(1)} %copy-done.2, ...), custom_call_target="tpu_custom_call" | custom-call | flops 67108864 | bytes 1048576 | tf_op jit(solution)/shard_map/pallas_call | solution.py:606
  39.5 1.6 %collective-permute-start.6 = (bf16[32,5120]{1,0:T(8,128)(2,1)S(1)}, bf16[32,5120]{1,0:T(8,128)(2,1)S(1)}, u32[]{:S(2)}, u32[]{:S(2)}) collective-permute-start(bf16[32,5120]{1,0:T(8,128)(2,1)S(1)} %get-tuple-element.32), channel_id=1, source_target_pairs={{0,1},{1,0},{2,3},{3,2},{4,5},{5,4},{6,7},{7,6},{8,9},{9,8},{10,11... | collective-permute-start | bytes 983048 | tf_op jit(solution)/shard_map/ppermute | solution.py:623
  41.1 0.0 collective-permute-done.12.halo_ref
  41.1 5.0 %shard_map.44.fine_ref = f32[64,64,128]{2,1,0:T(8,128)S(1)} custom-call(bf16[80,80,128]{2,1,0:T(8,128)(2,1)S(1)} %pad_maximum_fusion.wide_ref, bf16[16,6400]{1,0:T(8,128)(2,1)S(1)} %collective-permute-done.12.halo_ref, bf16[640,512]{1,0:T(8,128)(2,1)S(1)} %get-tuple-element.33.lanes_ref, bf16[16,128,256]{2,1,0:T(8,128)(2,1)S(1)} %get-tuple-element.34.band_ref), custom_call_target="tpu_custom_call" | custom-call | flops 4294967296 | bytes 1048576 | tf_op jit(solution)/shard_map/pallas_call | solution.py:606
  46.1 0.0 collective-permute-done.7.slab_ref
  46.1 3.0 %shard_map.45.middle_ref = f32[48,48,128]{2,1,0:T(8,128)S(1)} custom-call(f32[3264,128]{1,0:T(8,128)S(1)} %get-tuple-element.35.flat_ref, bf16[24,2944]{1,0:T(8,128)(2,1)S(1)} %collective-permute-done.7.slab_ref, bf16[640,512]{1,0:T(8,128)(2,1)S(1)} %get-tuple-element.33.lanes_ref, bf16[16,128,256]{2,1,0:T(8,128)(2,1)S(1)} %get-tuple-element.34.band_ref, ...), custom_call_target="tpu_custom_call" | custom-call | flops 2147483648 | bytes 1048576 | tf_op jit(solution)/shard_map/pallas_call | solution.py:606
  49.1 1.5 %collective-permute-done.6.slab_ref = bf16[32,5120]{1,0:T(8,128)(2,1)S(1)} collective-permute-done((bf16[32,5120]{1,0:T(8,128)(2,1)S(1)}, bf16[32,5120]{1,0:T(8,128)(2,1)S(1)}, u32[]{:S(2)}, u32[]{:S(2)}) %collective-permute-start.6) | collective-permute-done | bytes 327712 | tf_op jit(solution)/shard_map/ppermute | solution.py:623
  50.5 4.5 %shard_map.46 = bf16[64,64,128]{2,1,0:T(8,128)(2,1)} custom-call(f32[2704,128]{1,0:T(8,128)S(1)} %get-tuple-element.31.flat_ref, bf16[32,5120]{1,0:T(8,128)(2,1)S(1)} %collective-permute-done.6.slab_ref, bf16[640,512]{1,0:T(8,128)(2,1)S(1)} %get-tuple-element.33.lanes_ref, bf16[16,128,256]{2,1,0:T(8,128)(2,1)S(1)} %get-tuple-element.34.band_ref, ...), custom_call_target="tpu_custom_call" | custom-call | flops 1073741824 | bytes 1048576 | tf_op jit(solution)/shard_map/pallas_call | solution.py:606
  (6 shorter events, 0.1 us)
Async XLA Ops:
  0.0 1.2 %copy-start = (bf16[64,64,128]{2,1,0:T(8,128)(2,1)S(1)}, bf16[64,64,128]{2,1,0:T(8,128)(2,1)}, u32[]{:S(2)}) copy-start(bf16[64,64,128]{2,1,0:T(8,128)(2,1)} %charges_ref.3) | copy-start | bytes 3145732
  1.2 9.5 %collective-permute-start.8 = (bf16[8,64,128]{2,1,0:T(8,128)(2,1)S(1)}, bf16[8,64,128]{2,1,0:T(8,128)(2,1)S(1)}, u32[]{:S(2)}, u32[]{:S(2)}) collective-permute-start(bf16[8,64,128]{2,1,0:T(8,128)(2,1)S(1)} %get-tuple-element.37), channel_id=1, source_target_pairs={{0,8},{8,16},{16,24},{24,0},{1,9},{9,17},{17,25},{25,1},{2,10},{10... | collective-permute-start | bytes 393224 | tf_op jit(solution)/shard_map/ppermute | solution.py:623
  4.4 7.8 %collective-permute-start.9 = (bf16[8,64,128]{2,1,0:T(8,128)(2,1)S(1)}, bf16[8,64,128]{2,1,0:T(8,128)(2,1)S(1)}, u32[]{:S(2)}, u32[]{:S(2)}) collective-permute-start(bf16[8,64,128]{2,1,0:T(8,128)(2,1)S(1)} %get-tuple-element.38), channel_id=1, source_target_pairs={{0,24},{8,0},{16,8},{24,16},{1,25},{9,1},{17,9},{25,17},{2,26},{10... | collective-permute-start | bytes 393224 | tf_op jit(solution)/shard_map/ppermute | solution.py:623
  6.5 23.6 %copy-start.1 = (bf16[64,64,128]{2,1,0:T(8,128)(2,1)S(1)}, bf16[64,64,128]{2,1,0:T(8,128)(2,1)}, u32[]{:S(2)}) copy-start(bf16[64,64,128]{2,1,0:T(8,128)(2,1)} %charges_ref.3) | copy-start | bytes 3145732
  12.2 17.9 %collective-permute-start.11 = (bf16[80,8,128]{2,1,0:T(8,128)(2,1)S(1)}, bf16[80,8,128]{2,1,0:T(8,128)(2,1)S(1)}, u32[]{:S(2)}, u32[]{:S(2)}) collective-permute-start(bf16[80,8,128]{2,1,0:T(8,128)(2,1)S(1)} %pad_maximum_fusion.2), channel_id=1, source_target_pairs={{0,6},{2,0},{4,2},{6,4},{1,7},{3,1},{5,3},{7,5},{8,14},{10,8},{12,... | collective-permute-start | bytes 491528 | tf_op jit(solution)/shard_map/ppermute | solution.py:623
  12.8 17.3 %collective-permute-start.10 = (bf16[80,8,128]{2,1,0:T(8,128)(2,1)S(1)}, bf16[80,8,128]{2,1,0:T(8,128)(2,1)S(1)}, u32[]{:S(2)}, u32[]{:S(2)}) collective-permute-start(bf16[80,8,128]{2,1,0:T(8,128)(2,1)S(1)} %pad_maximum_fusion.1), channel_id=1, source_target_pairs={{0,2},{2,4},{4,6},{6,0},{1,3},{3,5},{5,7},{7,1},{8,10},{10,12},{12... | collective-permute-start | bytes 491528 | tf_op jit(solution)/shard_map/ppermute | solution.py:623
  15.8 12.1 %collective-permute-start = (bf16[624,128]{1,0:T(8,128)(2,1)S(1)}, bf16[624,128]{1,0:T(8,128)(2,1)S(1)}, u32[]{:S(2)}, u32[]{:S(2)}) collective-permute-start(bf16[624,128]{1,0:T(8,128)(2,1)S(1)} %get-tuple-element.24), channel_id=1, source_target_pairs={{0,8},{8,16},{16,24},{24,0},{1,9},{9,17},{17,25},{25,1},{2,10},{10... | collective-permute-start | bytes 479240 | tf_op jit(solution)/shard_map/ppermute | solution.py:623
  17.5 10.4 %collective-permute-start.1 = (bf16[624,128]{1,0:T(8,128)(2,1)S(1)}, bf16[624,128]{1,0:T(8,128)(2,1)S(1)}, u32[]{:S(2)}, u32[]{:S(2)}) collective-permute-start(bf16[624,128]{1,0:T(8,128)(2,1)S(1)} %get-tuple-element.25), channel_id=1, source_target_pairs={{0,24},{8,0},{16,8},{24,16},{1,25},{9,1},{17,9},{25,17},{2,26},{10... | collective-permute-start | bytes 479240 | tf_op jit(solution)/shard_map/ppermute | solution.py:623
  19.7 8.2 %collective-permute-start.2 = (f32[3,16,128]{2,1,0:T(8,128)S(1)}, f32[3,16,128]{2,1,0:T(8,128)S(1)}, u32[]{:S(2)}, u32[]{:S(2)}) collective-permute-start(f32[3,16,128]{2,1,0:T(8,128)S(1)} %get-tuple-element.26), channel_id=1, source_target_pairs={{0,16},{8,24},{16,0},{24,8},{1,17},{9,25},{17,1},{25,9},{2,18},{10... | collective-permute-start | bytes 73736 | tf_op jit(solution)/shard_map/ppermute | solution.py:623
  28.3 9.7 %collective-permute-start.3 = (bf16[1008,128]{1,0:T(8,128)(2,1)S(1)}, bf16[1008,128]{1,0:T(8,128)(2,1)S(1)}, u32[]{:S(2)}, u32[]{:S(2)}) collective-permute-start(bf16[1008,128]{1,0:T(8,128)(2,1)S(1)} %get-tuple-element.28), channel_id=1, source_target_pairs={{0,2},{2,4},{4,6},{6,0},{1,3},{3,5},{5,7},{7,1},{8,10},{10,12},{12... | collective-permute-start | bytes 774152 | tf_op jit(solution)/shard_map/ppermute | solution.py:623
  28.3 9.7 %collective-permute-start.4 = (bf16[1008,128]{1,0:T(8,128)(2,1)S(1)}, bf16[1008,128]{1,0:T(8,128)(2,1)S(1)}, u32[]{:S(2)}, u32[]{:S(2)}) collective-permute-start(bf16[1008,128]{1,0:T(8,128)(2,1)S(1)} %get-tuple-element.29), channel_id=1, source_target_pairs={{0,6},{2,0},{4,2},{6,4},{1,7},{3,1},{5,3},{7,5},{8,14},{10,8},{12,... | collective-permute-start | bytes 774152 | tf_op jit(solution)/shard_map/ppermute | solution.py:623
  30.3 3.6 %copy-start.3 = (f32[4,4,17]{2,1,0:T(4,128)S(1)}, f32[4,4,17]{2,1,0:T(4,128)}, u32[]{:S(2)}) copy-start(f32[4,4,17]{2,1,0:T(4,128)} %param.4) | copy-start | bytes 3268
  30.3 7.7 %copy-start.2 = (bf16[1168,128]{1,0:T(8,128)(2,1)S(1)}, bf16[1168,128]{1,0:T(8,128)(2,1)}, u32[]{:S(2)}) copy-start(bf16[1168,128]{1,0:T(8,128)(2,1)} %constant.2.clone.table_ref) | copy-start | bytes 897028
  30.9 10.2 %collective-permute-start.12 = (bf16[16,6400]{1,0:T(8,128)(2,1)S(1)}, bf16[16,6400]{1,0:T(8,128)(2,1)S(1)}, u32[]{:S(2)}, u32[]{:S(2)}) collective-permute-start(bf16[16,6400]{1,0:T(8,128)(2,1)S(1)} %shard_map.43), channel_id=1, source_target_pairs={{0,1},{1,0},{2,3},{3,2},{4,5},{5,4},{6,7},{7,6},{8,9},{9,8},{10,11... | collective-permute-start | bytes 614408 | tf_op jit(solution)/shard_map/ppermute | solution.py:623
  32.4 6.5 %collective-permute-start.5 = (f32[5,16,128]{2,1,0:T(8,128)S(1)}, f32[5,16,128]{2,1,0:T(8,128)S(1)}, u32[]{:S(2)}, u32[]{:S(2)}) collective-permute-start(f32[5,16,128]{2,1,0:T(8,128)S(1)} %get-tuple-element.30), channel_id=1, source_target_pairs={{0,4},{2,6},{4,0},{6,2},{1,5},{3,7},{5,1},{7,3},{8,12},{10,14},{12... | collective-permute-start | bytes 122888 | tf_op jit(solution)/shard_map/ppermute | solution.py:623
  38.4 7.7 %collective-permute-start.7 = (bf16[24,2944]{1,0:T(8,128)(2,1)S(1)}, bf16[24,2944]{1,0:T(8,128)(2,1)S(1)}, u32[]{:S(2)}, u32[]{:S(2)}) collective-permute-start(bf16[24,2944]{1,0:T(8,128)(2,1)S(1)} %get-tuple-element.36), channel_id=1, source_target_pairs={{0,1},{1,0},{2,3},{3,2},{4,5},{5,4},{6,7},{7,6},{8,9},{9,8},{10,11... | collective-permute-start | bytes 423944 | tf_op jit(solution)/shard_map/ppermute | solution.py:623
  39.5 11.0 %collective-permute-start.6 = (bf16[32,5120]{1,0:T(8,128)(2,1)S(1)}, bf16[32,5120]{1,0:T(8,128)(2,1)S(1)}, u32[]{:S(2)}, u32[]{:S(2)}) collective-permute-start(bf16[32,5120]{1,0:T(8,128)(2,1)S(1)} %get-tuple-element.32), channel_id=1, source_target_pairs={{0,1},{1,0},{2,3},{3,2},{4,5},{5,4},{6,7},{7,6},{8,9},{9,8},{10,11... | collective-permute-start | bytes 983048 | tf_op jit(solution)/shard_map/ppermute | solution.py:623
